TPU v7x, 32 devices: a whole 2x2x4 slice. The times are simulated.
32 devices in a mesh: ens: 4 (over y, x), lat: 2 (over core), lon: 4 (over z).
Axes of the slice: x: 2, y: 2, z: 4, core: 2. Of those that a mesh axis runs over, the one named last changes fastest.
Arguments:
- fields: bfloat16 [8, 36, 96, 384], P('ens', 'lat', 'lon'), parts along dimension 0, may hold values from -6 to 6
- region_ids: int32 [2, 36, 96], P(None, 'lat', 'lon'), may hold values from 0 to 3
- bias_index: int32 [144, 144], replicated, may hold values from 0 to 3311
- earth_bias: bfloat16 [6, 3312, 12], P('lat'), may hold values from -70 to 170
- w_qkv: bfloat16 [384, 1152], replicated, may hold values from -0.3125 to 0.3125
- w_proj: bfloat16 [384, 384], replicated, may hold values from -0.3125 to 0.3125
- w_fc1: bfloat16 [384, 1536], replicated, may hold values from -0.3125 to 0.3125
- w_fc2: bfloat16 [1536, 384], replicated, may hold values from -0.15625 to 0.15625
Outputs:
- result: bfloat16 [8, 36, 96, 384], P('ens', 'lat', 'lon'), parts along dimension 0
There are 4 independent parts, one for each index of `ens`. A program takes and returns all parts, laid end to end along the dimension named above; an argument that names none is the same for every part. Nothing has to cross between parts.
All inputs are finite; a program needn't handle non-finite values.
Results may differ from a plain program's by a relative error of at most 0.009.
Values may be sent and summed in bfloat16 or wider, within the bound.
A program may use at most 128 MiB of HBM per device.

v0:
```python
import jax
import jax.numpy as jnp
from jax import lax
from jax.sharding import PartitionSpec as P

WZ = 2
WLAT = 6
WLON = 12


EPS_NORM = 1e-05


def from_behind(value, axis, steps):
    count = lax.axis_size(axis)
    pairs = [(source, (source + steps) % count) for source in range(count)]
    return lax.ppermute(value, axis, pairs)


def layer_norm(tokens_in):
    widened = tokens_in.astype(jnp.float32)
    average = jnp.mean(widened, axis=-1, keepdims=True)
    centred = widened - average
    spread = jnp.mean(centred * centred, axis=-1, keepdims=True)
    return (centred * lax.rsqrt(spread + EPS_NORM)).astype(jnp.bfloat16)


def bias_scores(earth_bias, bias_index):
    bands, positions, head_count = earth_bias.shape
    window_tokens = bias_index.shape[0]
    flat_table = earth_bias.transpose(0, 2, 1).reshape(bands * head_count, positions)
    picked = jnp.take(flat_table, bias_index.reshape(-1), axis=1)
    return picked.astype(jnp.float32).reshape(bands, head_count, window_tokens, window_tokens)


def attend(normed, region_block, bias_table, w_qkv, w_proj):
    levels, lat_rows, lon_cols, feature_width = normed.shape
    lat_wins = lat_rows // WLAT
    lon_wins = lon_cols // WLON
    window_tokens = levels * WLAT * WLON
    head_count = bias_table.shape[1]
    head_dim = feature_width // head_count
    windowed = normed.reshape(levels, lat_wins, WLAT, lon_wins, WLON, feature_width)
    windowed = windowed.transpose(1, 3, 0, 2, 4, 5).reshape(-1, feature_width)
    packed = jnp.dot(windowed, w_qkv, preferred_element_type=jnp.float32).astype(jnp.bfloat16)
    packed = packed.reshape(lat_wins, lon_wins, window_tokens, 3, head_count, head_dim)
    queries = packed[:, :, :, 0]
    key_rows = packed[:, :, :, 1]
    value_rows = packed[:, :, :, 2]
    regions = region_block.reshape(levels, lat_wins, WLAT, lon_wins, WLON)
    regions = regions.transpose(1, 3, 0, 2, 4).reshape(lat_wins, lon_wins, window_tokens)
    scores = jnp.einsum("abihd,abjhd->abhij", queries, key_rows, preferred_element_type=jnp.float32)
    scores = scores * head_dim ** (-0.5) + bias_table[:, None]
    allowed = regions[:, :, :, None] == regions[:, :, None, :]
    scores = jnp.where(allowed[:, :, None], scores, -jnp.inf)
    maxima = jnp.max(scores, axis=-1, keepdims=True)
    exponent = jnp.exp(scores - maxima)
    attn_weights = (exponent / jnp.sum(exponent, axis=-1, keepdims=True)).astype(jnp.bfloat16)
    context = jnp.einsum(
        "abhij,abjhd->abihd", attn_weights, value_rows, preferred_element_type=jnp.float32
    )
    context = context.astype(jnp.bfloat16).reshape(-1, feature_width)
    projected = jnp.dot(context, w_proj, preferred_element_type=jnp.float32).astype(jnp.bfloat16)
    projected = projected.reshape(lat_wins, lon_wins, levels, WLAT, WLON, feature_width)
    return projected.transpose(2, 0, 3, 1, 4, 5).reshape(levels, lat_rows, lon_cols, feature_width)


def feed_forward(residual, w_fc1, w_fc2):
    feature_width = residual.shape[-1]
    normed = layer_norm(residual).reshape(-1, feature_width)
    hidden = jax.nn.gelu(
        jnp.dot(normed, w_fc1, preferred_element_type=jnp.float32), approximate=False
    )
    hidden = hidden.astype(jnp.bfloat16)
    summed = residual.reshape(-1, feature_width).astype(jnp.float32) + jnp.dot(
        hidden, w_fc2, preferred_element_type=jnp.float32
    )
    return summed.astype(jnp.bfloat16).reshape(residual.shape)


def forward_shift(source):
    half_lev = WZ // 2
    half_lat = WLAT // 2
    half_lon = WLON // 2
    arrived = from_behind(source[:, :, :half_lon], "lon", -1)
    along_lon = jnp.concatenate([source[:, :, half_lon:], arrived], axis=2)
    rows_sent = from_behind(along_lon[:, :half_lat], "lat", -1)
    along_lat = jnp.concatenate([along_lon[:, half_lat:], rows_sent], axis=1)
    return jnp.roll(along_lat, -half_lev, axis=0)


def backward_shift(shifted_result):
    half_lev = WZ // 2
    half_lat = WLAT // 2
    half_lon = WLON // 2
    rolled = jnp.roll(shifted_result, half_lev, axis=0)
    rows_back = from_behind(rolled[:, -half_lat:], "lat", 1)
    along_lat = jnp.concatenate([rows_back, rolled[:, :-half_lat]], axis=1)
    cols_back = from_behind(along_lat[:, :, -half_lon:], "lon", 1)
    return jnp.concatenate([cols_back, along_lat[:, :, :-half_lon]], axis=2)


def local(fields, region_ids, bias_index, earth_bias, w_qkv, w_proj, w_fc1, w_fc2):
    bias_table = bias_scores(earth_bias, bias_index)
    source = layer_norm(fields)
    shifted = forward_shift(source)
    attn_out = attend(shifted, region_ids, bias_table, w_qkv, w_proj)
    returned = backward_shift(attn_out)
    residual = (fields.astype(jnp.float32) + returned.astype(jnp.float32)).astype(jnp.bfloat16)
    return feed_forward(residual, w_fc1, w_fc2)


def solution(mesh):
    return jax.shard_map(
        local,
        mesh=mesh,
        in_specs=(
            P("ens", "lat", "lon", None),
            P(None, "lat", "lon"),
            P(),
            P("lat", None, None),
            P(),
            P(),
            P(),
            P(),
        ),
        out_specs=P("ens", "lat", "lon", None),
        check_vma=False,
    )
```

profile of v0, /device:TPU:0, one launch (start us, length us, event | category | flops | bytes accessed | tf_op | source)
XLA Modules:
  0.0 148.7 jit_solution(272674584063061277)
XLA Ops:
  0.0 1.4 convert_reduce_fusion
  1.4 1.5 fusion.26
  2.9 1.4 fusion.27
  5.0 5.1 %collective-permute-start = (bf16[2,18,6,384]{3,2,1,0:T(8,128)(2,1)}, bf16[2,18,6,384]{3,2,1,0:T(8,128)(2,1)}, u32[]{:S(2)}, u32[]{:S(2)}) collective-permute-start(bf16[2,18,6,384]{3,2,1,0:T(8,128)(2,1)} %slice.75), channel_id=1, source_target_pairs={{0,3},{1,0},{2,1},{3,2},{4,7},{5,4},{6,5},{7,6},{8,11},{9,8},{10,9... | collective-permute-start | bytes 497672 | tf_op jit(solution)/shard_map/ppermute | solution.py:17
  11.0 1.1 reshape.114
  13.6 1.1 reshape.113
  15.1 42.0 %gather_fusion = bf16[20736,36]{1,0:T(8,128)(2,1)} fusion(bf16[36,3312]{0,1:T(8,128)(2,1)S(1)} %copy.25, s32[21504]{0:T(1024)S(1)} %pad_clamp_fusion), kind=kCustom, calls=%fused_computation | custom fusion | bytes 3068928 | tf_op jit(solution)/shard_map/jit(_take)/gather | solution.py:32
  57.1 5.1 %copy.26 = bf16[36,20736]{1,0:T(8,128)(2,1)S(1)} copy(bf16[36,20736]{0,1:T(8,128)(2,1)} %bitcast.53) | data formatting | bytes 2985984 | tf_op jit(solution)/shard_map/jit(_take)/gather | solution.py:32
  62.3 6.6 %gather.7 = bf16[3,12,144,144]{3,2,1,0:T(8,128)(2,1)} reshape(bf16[36,20736]{1,0:T(8,128)(2,1)S(1)} %copy.26) | data formatting | bytes 2985984 | tf_op jit(solution)/shard_map/jit(_take)/gather | solution.py:32
  68.9 4.4 %select_convert_fusion = f32[3,12,144,144]{3,2,1,0:T(8,128)} fusion(bf16[3,12,144,144]{3,2,1,0:T(8,128)(2,1)} %gather.7, pred[144,144]{1,0:T(8,128)(4,1)S(1)} %compare_and_fusion), kind=kLoop, calls=%fused_computation.32 | loop fusion | flops 1492992 | bytes 4499712 | tf_op jit(solution)/shard_map/convert_element_type | solution.py:33
  73.3 6.6 %copy.27 = f32[3,12,144,144]{2,3,1,0:T(8,128)} copy(f32[3,12,144,144]{3,2,1,0:T(8,128)} %select_convert_fusion) | data formatting | bytes 5971968 | tf_op jit(solution)/shard_map/convert_element_type | solution.py:33
  81.6 1.0 fusion.32
  83.9 3.7 %convolution_convert_fusion = bf16[864,1152]{1,0:T(8,128)(2,1)} fusion(bf16[864,384]{1,0:T(8,128)(2,1)S(1)} %reshape.110, bf16[384,1152]{1,0:T(8,128)(2,1)} %param.12), kind=kOutput, calls=%fused_computation.31 | convolution fusion | flops 765407232 | bytes 3538944 | tf_op jit(solution)/shard_map/dot_general | solution.py:45
  87.6 2.9 %copy.20 = bf16[864,1152]{0,1:T(8,128)(2,1)S(1)} copy(bf16[864,1152]{1,0:T(8,128)(2,1)} %convolution_convert_fusion) | data formatting | bytes 3981312 | tf_op jit(solution)/shard_map/convert_element_type | solution.py:45
  90.5 4.1 %reshape.111 = bf16[3,2,144,3,12,32]{2,1,0,5,4,3:T(2,128)(2,1)} reshape(bf16[864,1152]{0,1:T(8,128)(2,1)S(1)} %copy.20) | data formatting | bytes 3981312 | tf_op jit(solution)/shard_map/reshape | solution.py:46
  94.5 5.3 %fusion.68 = (bf16[3,2,144,1,12,32]{2,1,0,5,4,3:T(2,128)(2,1)S(1)}, bf16[3,2,144,1,12,32]{2,1,0,5,4,3:T(2,128)(2,1)S(1)}, bf16[3,2,144,1,12,32]{2,1,0,5,4,3:T(2,128)(2,1)}) fusion(bf16[3,2,144,3,12,32]{2,1,0,5,4,3:T(2,128)(2,1)} %reshape.111), kind=kLoop, calls=%fused_computation.111 | loop fusion | bytes 3981312 | tf_op jit(solution)/shard_map/slice | solution.py:49
  99.8 11.8 %fusion.70 = (f32[3,2,12,144]{3,2,1,0:T(8,128)}, f32[3,2,12,144,144]{3,4,2,1,0:T(8,128)}) fusion(f32[3,12,144,144]{2,3,1,0:T(8,128)} %copy.27, pred[3,2,144,144]{2,3,1,0:T(8,128)(4,1)} %broadcast_compare_fusion, bf16[3,2,144,1,12,32]{2,1,0,5,4,3:T(2,128)(2,1)S(1)} %get-tuple-element.8, bf16[3,2,144,1,12,32]{2,1,0,5,4,3:T(2,128)(2,1)} %get-tuple-element.9), kind=kOutput, calls=%fused_computation.113 | convolution fusion | flops 103016592 | bytes 10450944 | tf_op jit(solution)/shard_map/sub | solution.py:57
  111.6 4.9 %fusion.22 = bf16[3,2,144,12,32]{2,4,3,1,0:T(8,128)(2,1)S(1)} fusion(f32[3,2,12,144,144]{3,4,2,1,0:T(8,128)} %get-tuple-element.13, f32[3,2,12,144]{3,2,1,0:T(8,128)} %get-tuple-element.12, bf16[3,2,144,1,12,32]{2,1,0,5,4,3:T(2,128)(2,1)S(1)} %get-tuple-element.7), kind=kOutput, calls=%fused_computation.39 | convolution fusion | flops 98869248 | bytes 7340544 | tf_op jit(solution)/shard_map/abhij,abjhd->abihd/dot_general | solution.py:59
  116.5 1.2 copy.29
  118.4 1.4 convolution_convert_fusion.1
  119.8 1.3 reshape.116
  122.0 1.0 collective-permute-done.2
  123.3 9.4 %collective-permute-done.3 = bf16[2,18,6,384]{3,2,1,0:T(8,128)(2,1)S(1)} collective-permute-done((bf16[2,18,6,384]{3,2,1,0:T(8,128)(2,1)S(1)}, bf16[2,18,6,384]{3,2,1,0:T(8,128)(2,1)S(1)}, u32[]{:S(2)}, u32[]{:S(2)}) %collective-permute-start.3) | collective-permute-done | bytes 165920 | tf_op jit(solution)/shard_map/ppermute | solution.py:17
  133.9 14.8 %fusion.25 = bf16[864,384]{1,0:T(8,128)(2,1)} fusion(bf16[1536,384]{1,0:T(8,128)(2,1)S(1)} %copy-done, bf16[864,384]{1,0:T(8,128)(2,1)S(1)} %bitcast.57, bf16[384,1536]{1,0:T(8,128)(2,1)} %param.14, bf16[864,384]{1,0:T(8,128)(2,1)S(1)} %bitcast.54), kind=kOutput, calls=%fused_computation.42 | convolution fusion | flops 2125688832 | bytes 4349952 | tf_op jit(solution)/shard_map/dot_general | solution.py:75
  (45 shorter events, 9.4 us)
Async XLA Ops:
  0.0 133.9 %copy-start = (bf16[1536,384]{1,0:T(8,128)(2,1)S(1)}, bf16[1536,384]{1,0:T(8,128)(2,1)}, u32[]{:S(2)}) copy-start(bf16[1536,384]{1,0:T(8,128)(2,1)} %param.15) | copy-start | bytes 3538948
  5.0 75.8 %collective-permute-start = (bf16[2,18,6,384]{3,2,1,0:T(8,128)(2,1)}, bf16[2,18,6,384]{3,2,1,0:T(8,128)(2,1)}, u32[]{:S(2)}, u32[]{:S(2)}) collective-permute-start(bf16[2,18,6,384]{3,2,1,0:T(8,128)(2,1)} %slice.75), channel_id=1, source_target_pairs={{0,3},{1,0},{2,1},{3,2},{4,7},{5,4},{6,5},{7,6},{8,11},{9,8},{10,9... | collective-permute-start | bytes 497672 | tf_op jit(solution)/shard_map/ppermute | solution.py:17
  81.6 1.4 collective-permute-start.1
  111.6 6.8 %copy-start.2 = (bf16[384,384]{1,0:T(8,128)(2,1)S(1)}, bf16[384,384]{1,0:T(8,128)(2,1)}, u32[]{:S(2)}) copy-start(bf16[384,384]{1,0:T(8,128)(2,1)} %param.13) | copy-start | bytes 884740
  119.8 12.9 %copy-start.1 = (bf16[2,18,24,384]{3,2,1,0:T(8,128)(2,1)S(1)}, bf16[2,18,24,384]{3,2,1,0:T(8,128)(2,1)}, u32[]{:S(2)}) copy-start(bf16[2,18,24,384]{3,2,1,0:T(8,128)(2,1)} %param.8) | copy-start | bytes 1990660
  121.6 1.4 collective-permute-start.2
  123.0 9.7 %collective-permute-start.3 = (bf16[2,18,6,384]{3,2,1,0:T(8,128)(2,1)S(1)}, bf16[2,18,6,384]{3,2,1,0:T(8,128)(2,1)S(1)}, u32[]{:S(2)}, u32[]{:S(2)}) collective-permute-start(bf16[2,18,6,384]{3,2,1,0:T(8,128)(2,1)S(1)} %pad_maximum_fusion.2), channel_id=1, source_target_pairs={{0,1},{1,2},{2,3},{3,0},{4,5},{5,6},{6,7},{7,4},{8,9},{9,10},{10,1... | collective-permute-start | bytes 497672 | tf_op jit(solution)/shard_map/ppermute | solution.py:17
where the time goes:
time: 150 us; the launch traced here: 149 us
  local copies, waits for them, and re-layouts  81.5 us (54%)
  matrix products  36.7 us (24%)
  other arithmetic  13.9 us (9%)
  waiting for transfers between devices  10.6 us (7%)
  starting transfers between devices  5.74 us (4%)
    gather x3, local copies, waits for them, and re-layouts, bias_scores(): picked = jnp.take(flat_table, bias_index.reshape(-1), axis=1)  53.8 us
    dot_general x1, matrix products, feed_forward(): jnp.dot(hidden, w_fc2, preferred_element_type=jnp.float32)  14.8 us
    sub x1, matrix products, attend(): exponent = jnp.exp(scores - maxima)  11.8 us
    ppermute x4, waiting for transfers between devices, from_behind(): return lax.ppermute(value, axis, pairs)  10.6 us
    convert_element_type x1, local copies, waits for them, and re-layouts, bias_scores(): picked.astype(jnp.float32)  6.6 us
    ppermute x4, starting transfers between devices, from_behind(): return lax.ppermute(value, axis, pairs)  5.74 us
    slice x1, local copies, waits for them, and re-layouts, attend(): value_rows = packed[:, :, :, 2]  5.26 us
    dot_general x1, matrix products, attend(): jnp.einsum('abhij,abjhd->abihd', attn_weights, value_rows, preferred_elem...  4.93 us
  transfers between devices with their start and end apart: 4, of which 3 were waited for; matrix products, arithmetic and copies ran while one was open for 48% of the time, Pallas kernels for 0%

commit v1 on v0

v1 whole, which is shorter than its diff:
```python
import functools
import math

import jax
import jax.numpy as jnp
from jax import lax
from jax.experimental import pallas as pl
from jax.experimental.pallas import tpu as pltpu
from jax.sharding import PartitionSpec as P

WZ = 2
WLAT = 6
WLON = 12
EPS_NORM = 1e-05
LOG2E = math.log2(math.e)
LO = 256
LANES = 128
NT = (((1,), (1,)), ((), ()))


def norm_rows(wide):
    average = jnp.mean(wide, axis=-1, keepdims=True)
    centred = wide - average
    spread = jnp.mean(centred * centred, axis=-1, keepdims=True)
    return (centred * lax.rsqrt(spread + EPS_NORM)).astype(jnp.bfloat16)


def bias_kernel(slab, main_idx, rest_idx, table, main_out, rest_a, rest_b):
    tokens = main_idx.shape[0]
    rest = rest_idx.shape[0]
    pieces = table.shape[0] // slab
    low = lax.broadcasted_iota(jnp.int32, (LO, LANES), 0)

    def lookup(left, right):
        spots = [
            jnp.where(low == (row & (LO - 1)), 1.0, 0.0).astype(jnp.bfloat16)
            for row in (left, right)
        ]
        found = jnp.dot(
            table[...], jnp.concatenate(spots, axis=1), preferred_element_type=jnp.float32
        )
        picked = []
        for half, row in enumerate((left, right)):
            high = row // LO
            columns = found[:, half * LANES : (half + 1) * LANES]
            total = columns[(pieces - 1) * slab :]
            for piece in range(pieces - 1):
                total = jnp.where(high == piece, columns[piece * slab : (piece + 1) * slab], total)
            picked.append(total * LOG2E)
        return picked

    @pl.loop(0, tokens // 8)
    def _(block):
        rows = main_idx[pl.ds(pl.multiple_of(block * 8, 8), 8), :]
        for pair in range(4):
            first, second = lookup(rows[2 * pair : 2 * pair + 1], rows[2 * pair + 1 : 2 * pair + 2])
            key = block * 8 + 2 * pair
            main_out[pl.ds(key, slab, stride=tokens), :] = first
            main_out[pl.ds(key + 1, slab, stride=tokens), :] = second

    @pl.loop(0, rest // 8)
    def _(block):
        rows = rest_idx[pl.ds(pl.multiple_of(block * 8, 8), 8), :]
        for query in range(8):
            row = rows[query : query + 1]
            first, second = lookup(row[:, :LANES], row[:, LANES:])
            rest_a[pl.ds(block * 8 + query, slab, stride=rest), :] = first
            rest_b[pl.ds(block * 8 + query, slab, stride=rest), :] = second


def bias_tables(earth_bias, bias_index):
    bands, positions, heads = earth_bias.shape
    tokens = bias_index.shape[0]
    rest = tokens - LANES
    count = bands * heads
    slab = -(-count // 8) * 8
    pieces = -(-positions // LO)
    table = earth_bias.transpose(0, 2, 1).reshape(count, positions)
    table = jnp.pad(table, ((0, slab - count), (0, pieces * LO - positions)))
    table = table.reshape(slab, pieces, LO).transpose(1, 0, 2).reshape(pieces * slab, LO)
    main_idx = bias_index[:LANES].T
    rest_idx = jnp.pad(bias_index[LANES:], ((0, 0), (0, 2 * LANES - tokens)))
    return pl.pallas_call(
        functools.partial(bias_kernel, slab),
        out_shape=(
            jax.ShapeDtypeStruct((slab * tokens, LANES), jnp.float32),
            jax.ShapeDtypeStruct((slab * rest, LANES), jnp.float32),
            jax.ShapeDtypeStruct((slab * rest, LANES), jnp.float32),
        ),
        cost_estimate=pl.CostEstimate(
            flops=2 * table.size * tokens * tokens, bytes_accessed=slab * tokens * tokens * 4,
            transcendentals=0,
        ),
        name="bias_lookup",
    )(main_idx, rest_idx, table)


def attend_kernel(heads, x, reg_row, reg_col, bias_main, bias_a, bias_b, w_qkv, w_vt, w_proj, out, turned):
    tokens, width = x.shape[1:]
    dim = width // heads
    per = LANES // dim
    rest = tokens - LANES
    scale = dim ** (-0.5) * LOG2E
    normed = norm_rows(x[0].astype(jnp.float32))
    packed = jnp.dot(normed, w_qkv[:, : 2 * width], preferred_element_type=jnp.float32)
    packed = packed.astype(jnp.bfloat16)
    query, key = packed[:, :width], packed[:, width:]
    value_t = lax.dot_general(w_vt[...], normed, NT, preferred_element_type=jnp.float32)
    value_t = value_t.astype(jnp.bfloat16)
    row = reg_row[0]
    col = reg_col[0]
    barred = jnp.where(col == row[:, :LANES], 0.0, -jnp.inf)
    owner = lax.broadcasted_iota(jnp.int32, (LANES, LANES), 1) // dim
    zero = jnp.zeros((), jnp.bfloat16)
    for group in range(width // LANES):
        span = slice(group * LANES, (group + 1) * LANES)
        asked = query[:LANES, span]
        stacked = jnp.concatenate([jnp.where(owner == h, asked, zero) for h in range(per)], axis=0)
        raw = lax.dot_general(key[:, span], stacked, NT, preferred_element_type=jnp.float32)
        for h in range(per):
            head = group * per + h
            scores = raw[:, h * LANES : (h + 1) * LANES] * scale
            scores = scores + bias_main[head * tokens : (head + 1) * tokens, :] + barred
            grown = jnp.exp2(scores - jnp.max(scores, axis=0, keepdims=True))
            total = jnp.sum(grown, axis=0, keepdims=True)
            mixed = jnp.dot(
                value_t[head * dim : (head + 1) * dim],
                grown.astype(jnp.bfloat16),
                preferred_element_type=jnp.float32,
            )
            turned[head * dim : (head + 1) * dim, :] = mixed / total
    owner = lax.broadcasted_iota(jnp.int32, (rest, width), 1) // dim
    asked = query[LANES:]
    stacked = jnp.concatenate([jnp.where(owner == h, asked, zero) for h in range(heads)], axis=0)
    scores = lax.dot_general(stacked, key, NT, preferred_element_type=jnp.float32) * scale
    scores = scores + jnp.concatenate([bias_a[...], bias_b[:, : tokens - LANES]], axis=1)
    barred = jnp.where(col[LANES:] == row, 0.0, -jnp.inf)
    scores = scores + jnp.concatenate([barred] * heads, axis=0)
    grown = jnp.exp2(scores - jnp.max(scores, axis=1, keepdims=True))
    total = jnp.sum(grown, axis=1, keepdims=True)
    mixed = lax.dot_general(
        grown.astype(jnp.bfloat16), value_t, NT, preferred_element_type=jnp.float32
    )
    mixed = mixed / total
    last = jnp.zeros((rest, width), jnp.float32)
    for h in range(heads):
        last = jnp.where(owner == h, mixed[h * rest : (h + 1) * rest], last)
    context = jnp.concatenate([turned[...].T, last], axis=0).astype(jnp.bfloat16)
    out[0] = jnp.dot(context, w_proj[...], preferred_element_type=jnp.float32).astype(jnp.bfloat16)


def attend(windows, regions, tables, heads, per_band, w_qkv, w_proj):
    count, tokens, width = windows.shape
    rest = tokens - LANES
    whole = lambda w: (0, 0)
    band = lambda w: (w // per_band, 0)
    return pl.pallas_call(
        functools.partial(attend_kernel, heads),
        grid=(count,),
        out_shape=jax.ShapeDtypeStruct(windows.shape, jnp.bfloat16),
        in_specs=[
            pl.BlockSpec((1, tokens, width), lambda w: (w, 0, 0)),
            pl.BlockSpec((1, 1, tokens), lambda w: (w, 0, 0)),
            pl.BlockSpec((1, tokens, 1), lambda w: (w, 0, 0)),
            pl.BlockSpec((heads * tokens, LANES), band),
            pl.BlockSpec((heads * rest, LANES), band),
            pl.BlockSpec((heads * rest, LANES), band),
            pl.BlockSpec(w_qkv.shape, whole),
            pl.BlockSpec(w_proj.shape, whole),
            pl.BlockSpec(w_proj.shape, whole),
        ],
        out_specs=pl.BlockSpec((1, tokens, width), lambda w: (w, 0, 0)),
        scratch_shapes=[pltpu.VMEM((width, LANES), jnp.float32)],
        cost_estimate=pl.CostEstimate(
            flops=8 * count * tokens * width * width, bytes_accessed=windows.size * 4,
            transcendentals=count * heads * tokens * tokens,
        ),
        name="window_attention",
    )(
        windows, regions[:, None, :], regions[:, :, None], *tables,
        w_qkv, w_qkv[:, 2 * width :].T, w_proj,
    )


def forward_kernel(fields, returned, w_fc1, w_fc2, out):
    residual = fields[...].astype(jnp.float32) + returned[...].astype(jnp.float32)
    residual = residual.astype(jnp.bfloat16).astype(jnp.float32)
    normed = norm_rows(residual)
    grown = jnp.dot(normed, w_fc1[...], preferred_element_type=jnp.float32)
    hidden = (0.5 * grown * (1.0 + lax.erf(grown * math.sqrt(0.5)))).astype(jnp.bfloat16)
    summed = residual + jnp.dot(hidden, w_fc2[...], preferred_element_type=jnp.float32)
    out[...] = summed.astype(jnp.bfloat16)


def feed_forward(fields, returned, w_fc1, w_fc2, steps):
    rows, width = fields.shape
    tile = rows // steps
    block = pl.BlockSpec((tile, width), lambda r: (r, 0))
    whole = lambda r: (0, 0)
    return pl.pallas_call(
        forward_kernel,
        grid=(steps,),
        out_shape=jax.ShapeDtypeStruct(fields.shape, jnp.bfloat16),
        in_specs=[block, block, pl.BlockSpec(w_fc1.shape, whole), pl.BlockSpec(w_fc2.shape, whole)],
        out_specs=block,
        cost_estimate=pl.CostEstimate(
            flops=4 * rows * w_fc1.size, bytes_accessed=rows * width * 6,
            transcendentals=rows * w_fc1.shape[1],
        ),
        name="feed_forward",
    )(fields, returned, w_fc1, w_fc2)


def from_behind(value, axis, steps):
    count = lax.axis_size(axis)
    pairs = [(source, (source + steps) % count) for source in range(count)]
    return lax.ppermute(value, axis, pairs)


def from_corner(value, steps):
    lats, lons = lax.axis_size("lat"), lax.axis_size("lon")
    pairs = [
        (a * lons + o, (a + steps) % lats * lons + (o + steps) % lons)
        for a in range(lats)
        for o in range(lons)
    ]
    return lax.ppermute(value, ("lat", "lon"), pairs)


def forward_shift(source):
    half_lat = WLAT // 2
    half_lon = WLON // 2
    cols = from_behind(source[:, :, :half_lon], "lon", -1)
    rows = from_behind(source[:, :half_lat], "lat", -1)
    corner = from_corner(source[:, :half_lat, :half_lon], -1)
    top = jnp.concatenate([source[:, half_lat:, half_lon:], cols[:, half_lat:]], axis=2)
    bottom = jnp.concatenate([rows[:, :, half_lon:], corner], axis=2)
    return jnp.roll(jnp.concatenate([top, bottom], axis=1), -(WZ // 2), axis=0)


def backward_shift(shifted):
    half_lat = WLAT // 2
    half_lon = WLON // 2
    rolled = jnp.roll(shifted, WZ // 2, axis=0)
    cols = from_behind(rolled[:, :-half_lat, -half_lon:], "lon", 1)
    rows = from_behind(rolled[:, -half_lat:, :-half_lon], "lat", 1)
    corner = from_corner(rolled[:, -half_lat:, -half_lon:], 1)
    top = jnp.concatenate([corner, rows], axis=2)
    bottom = jnp.concatenate([cols, rolled[:, :-half_lat, :-half_lon]], axis=2)
    return jnp.concatenate([top, bottom], axis=1)


def local(fields, region_ids, bias_index, earth_bias, w_qkv, w_proj, w_fc1, w_fc2):
    levels, lat_rows, lon_cols, width = fields.shape
    lat_wins = lat_rows // WLAT
    lon_wins = lon_cols // WLON
    tokens = levels * WLAT * WLON
    tables = bias_tables(earth_bias, bias_index)
    shifted = forward_shift(fields)
    windows = shifted.reshape(levels, lat_wins, WLAT, lon_wins, WLON, width)
    windows = windows.transpose(1, 3, 0, 2, 4, 5).reshape(-1, tokens, width)
    regions = region_ids.reshape(levels, lat_wins, WLAT, lon_wins, WLON)
    regions = regions.transpose(1, 3, 0, 2, 4).reshape(-1, tokens)
    projected = attend(windows, regions, tables, earth_bias.shape[-1], lon_wins, w_qkv, w_proj)
    projected = projected.reshape(lat_wins, lon_wins, levels, WLAT, WLON, width)
    projected = projected.transpose(2, 0, 3, 1, 4, 5).reshape(fields.shape)
    returned = backward_shift(projected)
    result = feed_forward(
        fields.reshape(-1, width), returned.reshape(-1, width), w_fc1, w_fc2, lat_wins
    )
    return result.reshape(fields.shape)


def solution(mesh):
    return jax.shard_map(
        local,
        mesh=mesh,
        in_specs=(
            P("ens", "lat", "lon", None),
            P(None, "lat", "lon"),
            P(),
            P("lat", None, None),
            P(),
            P(),
            P(),
            P(),
        ),
        out_specs=P("ens", "lat", "lon", None),
        check_vma=False,
    )
```

time: 150 us -> 62.8 us (0.42)
  local copies, waits for them, and re-layouts: 81.5 us -> 12.4 us
  matrix products: 36.7 us -> 0 us
  Pallas kernels: 0 us -> 34.3 us
  other arithmetic: 13.9 us -> 1.35 us
  waiting for transfers between devices: 10.6 us -> 6.57 us
  starting transfers between devices: 5.74 us -> 7.61 us
    gather x3 -> x0, local copies, waits for them, and re-layouts: 53.8 us -> none  [bias_scores(): picked = jnp.take(flat_table, bias_index.reshape(-1), axis=1)]
    pallas_call x0 -> x3, Pallas kernels: none -> 34.3 us  [the longest x1 14 us: bias_tables(): pl.pallas_call(functools.partial(bias_kernel, slab), out_shape=(jax.Shape...]
    dot_general x4 -> x0, matrix products: 24.9 us -> none  [the longest x1 14.8 us: feed_forward(): jnp.dot(hidden, w_fc2, preferred_element_type=jnp.float32)]
    sub x1 -> x0, matrix products: 11.8 us -> none  [attend(): exponent = jnp.exp(scores - maxima)]
    convert_element_type x3 -> x0, local copies, waits for them, and re-layouts: 10.7 us -> none  [the longest x1 6.6 us: bias_scores(): picked.astype(jnp.float32)]
    ppermute x4, waiting for transfers between devices: 10.6 us -> 0.85 us  [from_behind(): return lax.ppermute(value, axis, pairs)]
    reshape x9 -> x6, local copies, waits for them, and re-layouts: 9.55 us -> 2.59 us  [the longest x1 1.21 us: local(): projected = projected.reshape(lat_wins, lon_wins, levels, WLAT, WLON, width)]
    convert_element_type x3 -> x0, other arithmetic: 6.1 us -> none  [the longest x1 4.41 us: bias_scores(): picked.astype(jnp.float32)]
  transfers between devices with their start and end apart: 4 -> 6, of which waited for: 3 -> 2; matrix products, arithmetic and copies ran while one was open for 48% -> 13% of each run, Pallas kernels for 0% -> 22%
where the time goes in v1:
time: 62.8 us; the launch traced here: 62.5 us
  Pallas kernels  34.3 us (55%)
  local copies, waits for them, and re-layouts  12.4 us (20%)
  starting transfers between devices  7.61 us (12%)
  waiting for transfers between devices  6.57 us (10%)
  other arithmetic  1.35 us (2%)
    pallas_call x1, Pallas kernels, bias_tables(): pl.pallas_call(functools.partial(bias_kernel, slab), out_shape=(jax.Shape...  14 us
    pallas_call x1, Pallas kernels, attend(): pl.pallas_call(functools.partial(attend_kernel, heads), grid=(count,), ou...  13.7 us
    pallas_call x1, Pallas kernels, feed_forward(): pl.pallas_call(forward_kernel, grid=(steps,), out_shape=jax.ShapeDtypeStr...  6.59 us
    ppermute x2, waiting for transfers between devices, from_corner(): return lax.ppermute(value, ('lat', 'lon'), pairs)  5.72 us
    ppermute x2, starting transfers between devices, from_corner(): return lax.ppermute(value, ('lat', 'lon'), pairs)  4.68 us
    ppermute x4, starting transfers between devices, from_behind(): return lax.ppermute(value, axis, pairs)  2.93 us
    unnamed x9, local copies, waits for them, and re-layouts  1.69 us
  transfers between devices with their start and end apart: 6, of which 2 were waited for; matrix products, arithmetic and copies ran while one was open for 13% of the time, Pallas kernels for 22%

profile of v1, /device:TPU:0, one launch (start us, length us, event | category | flops | bytes accessed | tf_op | source)
XLA Modules:
  0.0 62.5 jit_solution(5720795363839348893)
XLA Ops:
  0.0 0.8 %slice.66 = bf16[2,3,6,384]{3,2,1,0:T(8,128)(2,1)S(1)} slice(bf16[2,18,24,384]{3,2,1,0:T(8,128)(2,1)} %param.8), slice={[0:2], [0:3], [0:6], [0:384]} | slice | bytes 55296 | tf_op jit(solution)/shard_map/slice | solution.py:235
  0.8 4.5 %collective-permute-start.2 = (bf16[2,3,6,384]{3,2,1,0:T(8,128)(2,1)S(1)}, bf16[2,3,6,384]{3,2,1,0:T(8,128)(2,1)S(1)}, u32[]{:S(2)}, u32[]{:S(2)}) collective-permute-start(bf16[2,3,6,384]{3,2,1,0:T(8,128)(2,1)S(1)} %slice.66), channel_id=1, source_target_pairs={{0,7},{1,4},{2,5},{3,6},{4,3},{5,0},{6,1},{7,2},{8,15},{9,12},{10,... | collective-permute-start | bytes 82952 | tf_op jit(solution)/shard_map/ppermute | solution.py:227
  5.3 0.9 %slice.64 = bf16[2,3,24,384]{3,2,1,0:T(8,128)(2,1)S(1)} slice(bf16[2,18,24,384]{3,2,1,0:T(8,128)(2,1)} %param.8), slice={[0:2], [0:3], [0:24], [0:384]} | slice | bytes 221184 | tf_op jit(solution)/shard_map/slice | solution.py:234
  6.3 0.7 %collective-permute-start.1 = (bf16[2,3,24,384]{3,2,1,0:T(8,128)(2,1)S(1)}, bf16[2,3,24,384]{3,2,1,0:T(8,128)(2,1)S(1)}, u32[]{:S(2)}, u32[]{:S(2)}) collective-permute-start(bf16[2,3,24,384]{3,2,1,0:T(8,128)(2,1)S(1)} %slice.64), channel_id=1, source_target_pairs={{0,4},{4,0},{1,5},{5,1},{2,6},{6,2},{3,7},{7,3},{8,12},{12,8},{9,1... | collective-permute-start | bytes 331784 | tf_op jit(solution)/shard_map/ppermute | solution.py:217
  7.0 1.0 %slice.62 = bf16[2,18,6,384]{3,2,1,0:T(8,128)(2,1)S(1)} slice(bf16[2,18,24,384]{3,2,1,0:T(8,128)(2,1)} %param.8), slice={[0:2], [0:18], [0:6], [0:384]} | slice | bytes 331776 | tf_op jit(solution)/shard_map/slice | solution.py:233
  8.0 0.5 collective-permute-start
  8.5 0.9 %slice.69 = s32[128,144]{1,0:T(8,128)S(1)} slice(s32[144,144]{1,0:T(8,128)} %param.10), slice={[0:128], [0:144]} | slice | bytes 147456 | tf_op jit(solution)/shard_map/slice | solution.py:81
  9.4 0.7 %copy.25 = s32[128,144]{0,1:T(8,128)} copy(s32[128,144]{1,0:T(8,128)S(1)} %slice.69) | data formatting | bytes 147456
  10.2 0.2 reshape.38
  10.5 0.8 %copy.19 = bf16[13,40,256]{2,1,0:T(8,128)(2,1)} copy(bf16[13,40,256]{2,0,1:T(8,128)(2,1)S(1)} %bitcast.19) | data formatting | bytes 532480 | tf_op jit(solution)/shard_map/transpose | solution.py:80
  11.3 0.6 pad.8.rest_idx
  11.9 14.0 %bias_lookup.1 = (f32[5760,128]{1,0:T(8,128)}, f32[640,128]{1,0:T(8,128)}, f32[640,128]{1,0:T(8,128)}) custom-call(s32[144,128]{1,0:T(8,128)} %bitcast.27, s32[16,256]{1,0:T(8,128)} %pad.8.rest_idx, bf16[520,256]{1,0:T(8,128)(2,1)} %bitcast.26), custom_call_target="tpu_custom_call" | custom-call | flops 5520752640 | bytes 3317760 | tf_op jit(solution)/shard_map/bias_lookup/pallas_call | solution.py:83
  26.0 0.7 %broadcast_in_dim_reshape.8.reg_row = s32[6,1,144]{2,1,0:T(1,128)} reshape(s32[3,2,2,6,12]{4,3,2,1,0:T(8,128)S(1)} %bitcast.23) | data formatting | bytes 6912 | tf_op jit(solution)/shard_map/broadcast_in_dim;reshape | solution.py:180
  26.7 0.9 %broadcast_in_dim_reshape.9.reg_col = s32[6,144,1]{2,1,0:T(8,128)} reshape(s32[3,2,2,6,12]{4,3,2,1,0:T(8,128)S(1)} %bitcast.24) | data formatting | bytes 6912 | tf_op jit(solution)/shard_map/broadcast_in_dim;reshape | solution.py:180
  27.8 0.9 %copy.26 = bf16[384,384]{0,1:T(8,128)(2,1)} copy(bf16[384,384]{1,0:T(8,128)(2,1)S(1)} %slice-done) | data formatting | bytes 589824
  29.1 0.5 copy.15
  29.8 1.0 %reshape.35.x = bf16[6,144,384]{2,1,0:T(8,128)(2,1)} reshape(bf16[3,2,2,6,12,384]{5,4,3,2,1,0:T(8,128)(2,1)S(1)} %copy.16) | data formatting | bytes 1327104 | tf_op jit(solution)/shard_map/reshape | solution.py:261
  30.7 13.7 %window_attention.1 = bf16[6,144,384]{2,1,0:T(8,128)(2,1)} custom-call(bf16[6,144,384]{2,1,0:T(8,128)(2,1)} %reshape.35.x, s32[6,1,144]{2,1,0:T(1,128)} %broadcast_in_dim_reshape.8.reg_row, s32[6,144,1]{2,1,0:T(8,128)} %broadcast_in_dim_reshape.9.reg_col, f32[5760,128]{1,0:T(8,128)} %get-tuple-element.8.bias_main, f32[640,128]{1,0:T(8,128)} %get-tuple-element.9.bias_a, ...), custom_call_target="tpu_custom_call" | custom-call | flops 1019215872 | bytes 1327104 | tf_op jit(solution)/shard_map/window_attention/pallas_call | solution.py:157
  44.5 1.2 %reshape.40 = bf16[3,2,2,6,12,384]{5,4,3,2,1,0:T(8,128)(2,1)S(1)} reshape(bf16[6,144,384]{2,1,0:T(8,128)(2,1)} %window_attention.1) | data formatting | bytes 1327104 | tf_op jit(solution)/shard_map/reshape | solution.py:265
  46.2 1.6 %collective-permute-start.5 = (bf16[2,15,6,384]{3,2,1,0:T(8,128)(2,1)S(1)}, bf16[2,15,6,384]{3,2,1,0:T(8,128)(2,1)S(1)}, u32[]{:S(2)}, u32[]{:S(2)}) collective-permute-start(bf16[2,15,6,384]{3,2,1,0:T(8,128)(2,1)S(1)} %slice.88), channel_id=1, source_target_pairs={{0,1},{1,2},{2,3},{3,0},{4,5},{5,6},{6,7},{7,4},{8,9},{9,10},{10,1... | collective-permute-start | bytes 414728 | tf_op jit(solution)/shard_map/ppermute | solution.py:217
  48.2 5.7 %collective-permute-done.3 = bf16[2,3,6,384]{3,2,1,0:T(8,128)(2,1)S(1)} collective-permute-done((bf16[2,3,6,384]{3,2,1,0:T(8,128)(2,1)S(1)}, bf16[2,3,6,384]{3,2,1,0:T(8,128)(2,1)S(1)}, u32[]{:S(2)}, u32[]{:S(2)}) %collective-permute-start.3) | collective-permute-done | bytes 27680 | tf_op jit(solution)/shard_map/ppermute | solution.py:227
  53.9 0.8 %collective-permute-done.5 = bf16[2,15,6,384]{3,2,1,0:T(8,128)(2,1)S(1)} collective-permute-done((bf16[2,15,6,384]{3,2,1,0:T(8,128)(2,1)S(1)}, bf16[2,15,6,384]{3,2,1,0:T(8,128)(2,1)S(1)}, u32[]{:S(2)}, u32[]{:S(2)}) %collective-permute-start.5) | collective-permute-done | bytes 138272 | tf_op jit(solution)/shard_map/ppermute | solution.py:217
  54.8 1.1 %maximum_maximum_fusion.1 = bf16[2,18,24,384]{3,2,1,0:T(8,128)(2,1)} fusion(bf16[2,15,18,384]{3,2,1,0:T(8,128)(2,1)S(1)} %slice.89, bf16[2,15,6,384]{3,2,1,0:T(8,128)(2,1)S(1)} %collective-permute-done.5, bf16[2,3,18,384]{3,2,1,0:T(8,128)(2,1)S(1)} %collective-permute-done.4, bf16[2,3,6,384]{3,2,1,0:T(8,128)(2,1)S(1)} %collective-permute-done.3), kind=kLoop, calls=%fused_computation.2 | loop fusion | flops 2654208 | bytes 1327104 | tf_op jit(solution)/shard_map/concatenate | solution.py:250
  55.9 6.6 %feed_forward.1 = bf16[864,384]{1,0:T(8,128)(2,1)} custom-call(bf16[864,384]{1,0:T(8,128)(2,1)} %bitcast.20, bf16[864,384]{1,0:T(8,128)(2,1)} %bitcast.22, bf16[384,1536]{1,0:T(8,128)(2,1)} %w_fc1.1, bf16[1536,384]{1,0:T(8,128)(2,1)} %w_fc2.1), custom_call_target="tpu_custom_call" | custom-call | flops 2038431744 | bytes 1990656 | tf_op jit(solution)/shard_map/feed_forward/pallas_call | solution.py:200
  (38 shorter events, 1.7 us)
Async XLA Ops:
  0.0 10.1 %copy-start.1 = (bf16[3,3312,12]{1,2,0:T(8,128)(2,1)S(1)}, bf16[3,3312,12]{1,2,0:T(8,128)(2,1)}, u32[]{:S(2)}) copy-start(bf16[3,3312,12]{1,2,0:T(8,128)(2,1)} %param.11) | copy-start | bytes 715396
  0.8 28.0 %collective-permute-start.2 = (bf16[2,3,6,384]{3,2,1,0:T(8,128)(2,1)S(1)}, bf16[2,3,6,384]{3,2,1,0:T(8,128)(2,1)S(1)}, u32[]{:S(2)}, u32[]{:S(2)}) collective-permute-start(bf16[2,3,6,384]{3,2,1,0:T(8,128)(2,1)S(1)} %slice.66), channel_id=1, source_target_pairs={{0,7},{1,4},{2,5},{3,6},{4,3},{5,0},{6,1},{7,2},{8,15},{9,12},{10,... | collective-permute-start | bytes 82952 | tf_op jit(solution)/shard_map/ppermute | solution.py:227
  6.3 22.5 %collective-permute-start.1 = (bf16[2,3,24,384]{3,2,1,0:T(8,128)(2,1)S(1)}, bf16[2,3,24,384]{3,2,1,0:T(8,128)(2,1)S(1)}, u32[]{:S(2)}, u32[]{:S(2)}) collective-permute-start(bf16[2,3,24,384]{3,2,1,0:T(8,128)(2,1)S(1)} %slice.64), channel_id=1, source_target_pairs={{0,4},{4,0},{1,5},{5,1},{2,6},{6,2},{3,7},{7,3},{8,12},{12,8},{9,1... | collective-permute-start | bytes 331784 | tf_op jit(solution)/shard_map/ppermute | solution.py:217
  8.0 20.8 %collective-permute-start = (bf16[2,18,6,384]{3,2,1,0:T(8,128)(2,1)S(1)}, bf16[2,18,6,384]{3,2,1,0:T(8,128)(2,1)S(1)}, u32[]{:S(2)}, u32[]{:S(2)}) collective-permute-start(bf16[2,18,6,384]{3,2,1,0:T(8,128)(2,1)S(1)} %slice.62), channel_id=1, source_target_pairs={{0,3},{1,0},{2,1},{3,2},{4,7},{5,4},{6,5},{7,6},{8,11},{9,8},{10,9... | collective-permute-start | bytes 497672 | tf_op jit(solution)/shard_map/ppermute | solution.py:217
  8.5 2.8 %slice-start.1 = ((s32[144,144]{1,0:T(8,128)}), s32[16,144]{1,0:T(8,128)S(1)}, s32[]{:S(2)}) async-start(s32[144,144]{1,0:T(8,128)} %param.10), calls=%async_computation.1 | async-start | bytes 32768 | tf_op jit(solution)/shard_map/slice | solution.py:82
  11.9 14.0 %copy-start.2 = (s32[2,18,24]{2,0,1:T(2,128)S(1)}, s32[2,18,24]{2,0,1:T(2,128)}, u32[]{:S(2)}) copy-start(s32[2,18,24]{2,0,1:T(2,128)} %param.9) | copy-start | bytes 10372
  11.9 15.7 %copy-start = (bf16[2,18,24,384]{3,2,1,0:T(8,128)(2,1)S(1)}, bf16[2,18,24,384]{3,2,1,0:T(8,128)(2,1)}, u32[]{:S(2)}) copy-start(bf16[2,18,24,384]{3,2,1,0:T(8,128)(2,1)} %param.8) | copy-start | bytes 1990660
  25.9 1.9 %slice-start = ((bf16[384,1152]{1,0:T(8,128)(2,1)}), bf16[384,384]{1,0:T(8,128)(2,1)S(1)}, s32[]{:S(2)}) async-start(bf16[384,1152]{1,0:T(8,128)(2,1)} %w_qkv.1), calls=%async_computation | async-start | bytes 589824 | tf_op jit(solution)/shard_map/slice | solution.py:181
  46.2 8.5 %collective-permute-start.5 = (bf16[2,15,6,384]{3,2,1,0:T(8,128)(2,1)S(1)}, bf16[2,15,6,384]{3,2,1,0:T(8,128)(2,1)S(1)}, u32[]{:S(2)}, u32[]{:S(2)}) collective-permute-start(bf16[2,15,6,384]{3,2,1,0:T(8,128)(2,1)S(1)} %slice.88), channel_id=1, source_target_pairs={{0,1},{1,2},{2,3},{3,0},{4,5},{5,6},{6,7},{7,4},{8,9},{9,10},{10,1... | collective-permute-start | bytes 414728 | tf_op jit(solution)/shard_map/ppermute | solution.py:217
  47.9 6.1 %collective-permute-start.4 = (bf16[2,3,18,384]{3,2,1,0:T(8,128)(2,1)S(1)}, bf16[2,3,18,384]{3,2,1,0:T(8,128)(2,1)S(1)}, u32[]{:S(2)}, u32[]{:S(2)}) collective-permute-start(bf16[2,3,18,384]{3,2,1,0:T(8,128)(2,1)S(1)} %slice.87), channel_id=1, source_target_pairs={{0,4},{4,0},{1,5},{5,1},{2,6},{6,2},{3,7},{7,3},{8,12},{12,8},{9,1... | collective-permute-start | bytes 248840 | tf_op jit(solution)/shard_map/ppermute | solution.py:217
  48.0 6.0 %collective-permute-start.3 = (bf16[2,3,6,384]{3,2,1,0:T(8,128)(2,1)S(1)}, bf16[2,3,6,384]{3,2,1,0:T(8,128)(2,1)S(1)}, u32[]{:S(2)}, u32[]{:S(2)}) collective-permute-start(bf16[2,3,6,384]{3,2,1,0:T(8,128)(2,1)S(1)} %slice.86), channel_id=1, source_target_pairs={{0,5},{1,6},{2,7},{3,4},{4,1},{5,2},{6,3},{7,0},{8,13},{9,14},{10,... | collective-permute-start | bytes 82952 | tf_op jit(solution)/shard_map/ppermute | solution.py:227

commit v2 on v1

--- a/solution.py
+++ b/solution.py
@@ -15,6 +15,7 @@
 LOG2E = math.log2(math.e)
 LO = 256
 LANES = 128
+GRANT = 32 * 1024 * 1024
 NT = (((1,), (1,)), ((), ()))
 
 
@@ -91,24 +92,19 @@
             flops=2 * table.size * tokens * tokens, bytes_accessed=slab * tokens * tokens * 4,
             transcendentals=0,
         ),
+        compiler_params=pltpu.CompilerParams(vmem_limit_bytes=GRANT // 2),
         name="bias_lookup",
     )(main_idx, rest_idx, table)
 
 
-def attend_kernel(heads, x, reg_row, reg_col, bias_main, bias_a, bias_b, w_qkv, w_vt, w_proj, out, turned):
-    tokens, width = x.shape[1:]
+def attend_window(heads, normed, query, key, row, col, bias_main, bias_a, bias_b, w_vt, turned):
+    tokens, width = normed.shape
     dim = width // heads
     per = LANES // dim
     rest = tokens - LANES
     scale = dim ** (-0.5) * LOG2E
-    normed = norm_rows(x[0].astype(jnp.float32))
-    packed = jnp.dot(normed, w_qkv[:, : 2 * width], preferred_element_type=jnp.float32)
-    packed = packed.astype(jnp.bfloat16)
-    query, key = packed[:, :width], packed[:, width:]
     value_t = lax.dot_general(w_vt[...], normed, NT, preferred_element_type=jnp.float32)
     value_t = value_t.astype(jnp.bfloat16)
-    row = reg_row[0]
-    col = reg_col[0]
     barred = jnp.where(col == row[:, :LANES], 0.0, -jnp.inf)
     owner = lax.broadcasted_iota(jnp.int32, (LANES, LANES), 1) // dim
     zero = jnp.zeros((), jnp.bfloat16)
@@ -145,70 +141,69 @@
     last = jnp.zeros((rest, width), jnp.float32)
     for h in range(heads):
         last = jnp.where(owner == h, mixed[h * rest : (h + 1) * rest], last)
-    context = jnp.concatenate([turned[...].T, last], axis=0).astype(jnp.bfloat16)
-    out[0] = jnp.dot(context, w_proj[...], preferred_element_type=jnp.float32).astype(jnp.bfloat16)
-
-
-def attend(windows, regions, tables, heads, per_band, w_qkv, w_proj):
-    count, tokens, width = windows.shape
-    rest = tokens - LANES
-    whole = lambda w: (0, 0)
-    band = lambda w: (w // per_band, 0)
-    return pl.pallas_call(
-        functools.partial(attend_kernel, heads),
-        grid=(count,),
-        out_shape=jax.ShapeDtypeStruct(windows.shape, jnp.bfloat16),
-        in_specs=[
-            pl.BlockSpec((1, tokens, width), lambda w: (w, 0, 0)),
-            pl.BlockSpec((1, 1, tokens), lambda w: (w, 0, 0)),
-            pl.BlockSpec((1, tokens, 1), lambda w: (w, 0, 0)),
-            pl.BlockSpec((heads * tokens, LANES), band),
-            pl.BlockSpec((heads * rest, LANES), band),
-            pl.BlockSpec((heads * rest, LANES), band),
-            pl.BlockSpec(w_qkv.shape, whole),
-            pl.BlockSpec(w_proj.shape, whole),
-            pl.BlockSpec(w_proj.shape, whole),
-        ],
-        out_specs=pl.BlockSpec((1, tokens, width), lambda w: (w, 0, 0)),
-        scratch_shapes=[pltpu.VMEM((width, LANES), jnp.float32)],
-        cost_estimate=pl.CostEstimate(
-            flops=8 * count * tokens * width * width, bytes_accessed=windows.size * 4,
-            transcendentals=count * heads * tokens * tokens,
-        ),
-        name="window_attention",
-    )(
-        windows, regions[:, None, :], regions[:, :, None], *tables,
-        w_qkv, w_qkv[:, 2 * width :].T, w_proj,
-    )
-
-
-def forward_kernel(fields, returned, w_fc1, w_fc2, out):
-    residual = fields[...].astype(jnp.float32) + returned[...].astype(jnp.float32)
-    residual = residual.astype(jnp.bfloat16).astype(jnp.float32)
+    return jnp.concatenate([turned[...].T, last], axis=0).astype(jnp.bfloat16)
+
+
+def layer_kernel(heads, together, x, reg_row, reg_col, *refs):
+    biases, (w_qkv, w_vt, w_proj, w_fc1, w_fc2, out, turned) = refs[: 3 * together], refs[3 * together :]
+    tokens, width = x.shape[1:]
+    fields = x[...].reshape(together * tokens, width).astype(jnp.float32)
+    normed = norm_rows(fields)
+    packed = jnp.dot(normed, w_qkv[:, : 2 * width], preferred_element_type=jnp.float32)
+    packed = packed.astype(jnp.bfloat16)
+    contexts = []
+    for place in range(together):
+        rows = slice(place * tokens, (place + 1) * tokens)
+        contexts.append(
+            attend_window(
+                heads, normed[rows], packed[rows, :width], packed[rows, width:], reg_row[place],
+                reg_col[place], *biases[3 * place : 3 * place + 3], w_vt, turned.at[place],
+            )
+        )
+    context = jnp.concatenate(contexts, axis=0)
+    projected = jnp.dot(context, w_proj[...], preferred_element_type=jnp.float32)
+    projected = projected.astype(jnp.bfloat16).astype(jnp.float32)
+    residual = (fields + projected).astype(jnp.bfloat16).astype(jnp.float32)
     normed = norm_rows(residual)
     grown = jnp.dot(normed, w_fc1[...], preferred_element_type=jnp.float32)
     hidden = (0.5 * grown * (1.0 + lax.erf(grown * math.sqrt(0.5)))).astype(jnp.bfloat16)
     summed = residual + jnp.dot(hidden, w_fc2[...], preferred_element_type=jnp.float32)
-    out[...] = summed.astype(jnp.bfloat16)
-
-
-def feed_forward(fields, returned, w_fc1, w_fc2, steps):
-    rows, width = fields.shape
-    tile = rows // steps
-    block = pl.BlockSpec((tile, width), lambda r: (r, 0))
-    whole = lambda r: (0, 0)
+    out[...] = summed.astype(jnp.bfloat16).reshape(out.shape)
+
+
+def layer(windows, regions, tables, band_of, heads, w_qkv, w_vt, w_proj, w_fc1, w_fc2):
+    count, tokens, width = windows.shape
+    rest = tokens - LANES
+    together = 2 if count % 2 == 0 else 1
+    whole = lambda w: (0, 0)
+    bias_specs, bias_args = [], []
+    for place in range(together):
+        band = lambda w, place=place: (band_of(w * together + place), 0)
+        for table, rows in zip(tables, (tokens, rest, rest)):
+            bias_specs.append(pl.BlockSpec((heads * rows, LANES), band))
+            bias_args.append(table)
+    weights = (w_qkv, w_vt, w_proj, w_fc1, w_fc2)
     return pl.pallas_call(
-        forward_kernel,
-        grid=(steps,),
-        out_shape=jax.ShapeDtypeStruct(fields.shape, jnp.bfloat16),
-        in_specs=[block, block, pl.BlockSpec(w_fc1.shape, whole), pl.BlockSpec(w_fc2.shape, whole)],
-        out_specs=block,
+        functools.partial(layer_kernel, heads, together),
+        grid=(count // together,),
+        out_shape=jax.ShapeDtypeStruct(windows.shape, jnp.bfloat16),
+        in_specs=[
+            pl.BlockSpec((together, tokens, width), lambda w: (w, 0, 0)),
+            pl.BlockSpec((together, 1, tokens), lambda w: (w, 0, 0)),
+            pl.BlockSpec((together, tokens, 1), lambda w: (w, 0, 0)),
+            *bias_specs,
+            *[pl.BlockSpec(weight.shape, whole) for weight in weights],
+        ],
+        out_specs=pl.BlockSpec((together, tokens, width), lambda w: (w, 0, 0)),
+        scratch_shapes=[pltpu.VMEM((together, width, LANES), jnp.float32)],
+        compiler_params=pltpu.CompilerParams(vmem_limit_bytes=GRANT),
         cost_estimate=pl.CostEstimate(
-            flops=4 * rows * w_fc1.size, bytes_accessed=rows * width * 6,
-            transcendentals=rows * w_fc1.shape[1],
+            flops=2 * count * tokens * (w_qkv.size + w_proj.size + w_fc1.size + w_fc2.size) * 3,
+            bytes_accessed=windows.size * 4 + w_fc1.size * 8,
+            transcendentals=count * heads * tokens * tokens,
         ),
-        name="feed_forward",
-    )(fields, returned, w_fc1, w_fc2)
+        name="layer",
+    )(windows, regions[:, None, :], regions[:, :, None], *bias_args, *weights)
 
 
 def from_behind(value, axis, steps):
@@ -238,37 +233,53 @@
     return jnp.roll(jnp.concatenate([top, bottom], axis=1), -(WZ // 2), axis=0)
 
 
-def backward_shift(shifted):
-    half_lat = WLAT // 2
-    half_lon = WLON // 2
-    rolled = jnp.roll(shifted, WZ // 2, axis=0)
-    cols = from_behind(rolled[:, :-half_lat, -half_lon:], "lon", 1)
-    rows = from_behind(rolled[:, -half_lat:, :-half_lon], "lat", 1)
-    corner = from_corner(rolled[:, -half_lat:, -half_lon:], 1)
-    top = jnp.concatenate([corner, rows], axis=2)
-    bottom = jnp.concatenate([cols, rolled[:, :-half_lat, :-half_lon]], axis=2)
-    return jnp.concatenate([top, bottom], axis=1)
-
-
 def local(fields, region_ids, bias_index, earth_bias, w_qkv, w_proj, w_fc1, w_fc2):
     levels, lat_rows, lon_cols, width = fields.shape
     lat_wins = lat_rows // WLAT
     lon_wins = lon_cols // WLON
     tokens = levels * WLAT * WLON
+    half_lat = WLAT // 2
+    half_lon = WLON // 2
+    heads = earth_bias.shape[-1]
     tables = bias_tables(earth_bias, bias_index)
     shifted = forward_shift(fields)
     windows = shifted.reshape(levels, lat_wins, WLAT, lon_wins, WLON, width)
-    windows = windows.transpose(1, 3, 0, 2, 4, 5).reshape(-1, tokens, width)
+    windows = windows.transpose(1, 3, 0, 2, 4, 5).reshape(lat_wins, lon_wins, tokens, width)
     regions = region_ids.reshape(levels, lat_wins, WLAT, lon_wins, WLON)
-    regions = regions.transpose(1, 3, 0, 2, 4).reshape(-1, tokens)
-    projected = attend(windows, regions, tables, earth_bias.shape[-1], lon_wins, w_qkv, w_proj)
-    projected = projected.reshape(lat_wins, lon_wins, levels, WLAT, WLON, width)
-    projected = projected.transpose(2, 0, 3, 1, 4, 5).reshape(fields.shape)
-    returned = backward_shift(projected)
-    result = feed_forward(
-        fields.reshape(-1, width), returned.reshape(-1, width), w_fc1, w_fc2, lat_wins
+    regions = regions.transpose(1, 3, 0, 2, 4).reshape(lat_wins, lon_wins, tokens)
+    weights = (w_qkv, w_qkv[:, 2 * width :].T, w_proj, w_fc1, w_fc2)
+    edge_of = lambda a: jnp.concatenate([a[:-1, -1], a[-1]], axis=0)
+    edge = layer(
+        edge_of(windows), edge_of(regions), tables,
+        lambda w: jnp.minimum(w, lat_wins - 1), heads, *weights,
     )
-    return result.reshape(fields.shape)
+
+    def placed(block):
+        lats, lons = block.shape[:2]
+        block = block.reshape(lats, lons, levels, WLAT, WLON, width)
+        block = jnp.roll(block, WZ // 2, axis=2)
+        return block.transpose(2, 0, 3, 1, 4, 5).reshape(levels, lats * WLAT, lons * WLON, width)
+
+    right = placed(edge[: lat_wins - 1, None])
+    bottom = placed(edge[None, lat_wins - 1 :])
+    upper = lat_rows - WLAT
+    cols = jnp.concatenate([right[:, :, half_lon:], bottom[:, :half_lat, -half_lon:]], axis=1)
+    cols = from_behind(cols, "lon", 1)
+    rows = from_behind(bottom[:, half_lat:, :-half_lon], "lat", 1)
+    corner = from_corner(bottom[:, half_lat:, -half_lon:], 1)
+    right = right[:, :, :half_lon]
+    bottom = bottom[:, :half_lat, :-half_lon]
+    if lat_wins > 1 and lon_wins > 1:
+        inner_of = lambda a: a[:-1, :-1].reshape(-1, *a.shape[2:])
+        inner = layer(
+            inner_of(windows), inner_of(regions), tables,
+            lambda w: w // (lon_wins - 1), heads, *weights,
+        )
+        inner = placed(inner.reshape(lat_wins - 1, lon_wins - 1, tokens, width))
+        right = jnp.concatenate([inner, right], axis=2)
+    own = jnp.concatenate([right, bottom], axis=1)
+    own = jnp.concatenate([cols, own], axis=2)
+    return jnp.concatenate([jnp.concatenate([corner, rows], axis=2), own], axis=1)
 
 
 def solution(mesh):

time: 62.8 us -> 58.6 us (0.933)
  Pallas kernels: 34.3 us -> 25.3 us
  local copies, waits for them, and re-layouts: 12.4 us -> 19.3 us
  waiting for transfers between devices: 6.57 us -> 0.64 us
  other arithmetic: 1.35 us -> 5.12 us
    pallas_call x2, Pallas kernels: 20.3 us -> 13.2 us  [layer(): pl.pallas_call(functools.partial(layer_kernel, heads, together), grid=(co...]
    ppermute x2, waiting for transfers between devices: 5.72 us -> 0.01 us  [from_corner(): return lax.ppermute(value, ('lat', 'lon'), pairs)]
    ppermute x2, starting transfers between devices: 4.68 us -> 0.75 us  [from_corner(): return lax.ppermute(value, ('lat', 'lon'), pairs)]
    ppermute x4, starting transfers between devices: 2.93 us -> 6.71 us  [from_behind(): return lax.ppermute(value, axis, pairs)]
    reshape x2, local copies, waits for them, and re-layouts: 2.2 us -> 0.15 us  [the longest x1 0.09 us: local(): regions.transpose(1, 3, 0, 2, 4).reshape(lat_wins, lon_wins, tokens)]
    pallas_call x1, Pallas kernels: 14 us -> 12.1 us  [bias_tables(): pl.pallas_call(functools.partial(bias_kernel, slab), out_shape=(jax.Shape...]
    slice x1, local copies, waits for them, and re-layouts: 0.19 us -> 2.05 us  [forward_shift(): source[:, half_lat:, half_lon:]]
    concatenate x1 -> x3, other arithmetic: 1.14 us -> 2.89 us  [the longest x1 2.65 us: local(): jnp.concatenate([jnp.concatenate([corner, rows], axis=2), own], axis=1)]
  transfers between devices with their start and end apart: 6 -> 6, of which waited for: 2 -> 1; matrix products, arithmetic and copies ran while one was open for 13% -> 18% of each run, Pallas kernels for 22% -> 28%
where the time goes in v2:
time: 58.6 us; the launch traced here: 58.2 us
  Pallas kernels  25.3 us (43%)
  local copies, waits for them, and re-layouts  19.3 us (33%)
  starting transfers between devices  7.46 us (13%)
  other arithmetic  5.12 us (9%)
  waiting for transfers between devices  0.64 us (1%)
    pallas_call x2, Pallas kernels, layer(): pl.pallas_call(functools.partial(layer_kernel, heads, together), grid=(co...  13.2 us
    pallas_call x1, Pallas kernels, bias_tables(): pl.pallas_call(functools.partial(bias_kernel, slab), out_shape=(jax.Shape...  12.1 us
    ppermute x4, starting transfers between devices, from_behind(): return lax.ppermute(value, axis, pairs)  6.71 us
    unnamed x23, local copies, waits for them, and re-layouts  3.27 us
    concatenate x1, other arithmetic, local(): jnp.concatenate([jnp.concatenate([corner, rows], axis=2), own], axis=1)  2.65 us
    slice x1, local copies, waits for them, and re-layouts, forward_shift(): source[:, half_lat:, half_lon:]  2.05 us
    slice x1, local copies, waits for them, and re-layouts, forward_shift(): cols = from_behind(source[:, :, :half_lon], 'lon', -1)  1.69 us
    slice x1, local copies, waits for them, and re-layouts, forward_shift(): rows = from_behind(source[:, :half_lat], 'lat', -1)  1.56 us
  transfers between devices with their start and end apart: 6, of which 1 were waited for; matrix products, arithmetic and copies ran while one was open for 18% of the time, Pallas kernels for 28%

profile of v2, /device:TPU:0, one launch (start us, length us, event | category | flops | bytes accessed | tf_op | source)
XLA Modules:
  0.0 58.2 jit_solution(1251271291136379488)
XLA Ops:
  0.0 1.7 %slice.102 = bf16[2,18,6,384]{3,2,1,0:T(8,128)(2,1)} slice(bf16[2,18,24,384]{3,2,1,0:T(8,128)(2,1)} %param.8), slice={[0:2], [0:18], [0:6], [0:384]} | slice | bytes 331776 | tf_op jit(solution)/shard_map/slice | solution.py:228
  1.7 5.1 %collective-permute-start = (bf16[2,18,6,384]{3,2,1,0:T(8,128)(2,1)}, bf16[2,18,6,384]{3,2,1,0:T(8,128)(2,1)}, u32[]{:S(2)}, u32[]{:S(2)}) collective-permute-start(bf16[2,18,6,384]{3,2,1,0:T(8,128)(2,1)} %slice.102), channel_id=1, source_target_pairs={{0,3},{1,0},{2,1},{3,2},{4,7},{5,4},{6,5},{7,6},{8,11},{9,8},{10,9... | collective-permute-start | bytes 497672 | tf_op jit(solution)/shard_map/ppermute | solution.py:212
  6.8 1.6 %slice.104 = bf16[2,3,24,384]{3,2,1,0:T(8,128)(2,1)} slice(bf16[2,18,24,384]{3,2,1,0:T(8,128)(2,1)} %param.8), slice={[0:2], [0:3], [0:24], [0:384]} | slice | bytes 221184 | tf_op jit(solution)/shard_map/slice | solution.py:229
  8.3 1.4 %slice.106 = bf16[2,3,6,384]{3,2,1,0:T(8,128)(2,1)} slice(bf16[2,18,24,384]{3,2,1,0:T(8,128)(2,1)} %param.8), slice={[0:2], [0:3], [0:6], [0:384]} | slice | bytes 55296 | tf_op jit(solution)/shard_map/slice | solution.py:230
  9.7 0.6 collective-permute-start.2
  10.3 0.9 %reshape.39 = s32[2,3,6,2,12]{4,3,0,2,1:T(2,128)S(1)} reshape(s32[2,18,24]{2,0,1:T(2,128)} %param.9) | data formatting | bytes 6912 | tf_op jit(solution)/shard_map/reshape | solution.py:248
  11.9 12.1 %bias_lookup.1 = (f32[5760,128]{1,0:T(8,128)S(1)}, f32[640,128]{1,0:T(8,128)S(1)}, f32[640,128]{1,0:T(8,128)S(1)}) custom-call(s32[144,128]{1,0:T(8,128)S(1)} %bitcast.39, s32[16,256]{1,0:T(8,128)S(1)} %pad.8.rest_idx, bf16[520,256]{1,0:T(8,128)(2,1)S(1)} %bitcast.38), custom_call_target="tpu_custom_call" | custom-call | flops 5520752640 | bytes 3317760 | tf_op jit(solution)/shard_map/bias_lookup/pallas_call | solution.py:84
  24.0 0.7 %copy-done.1 = f32[640,128]{1,0:T(8,128)} copy-done((f32[640,128]{1,0:T(8,128)}, f32[640,128]{1,0:T(8,128)S(1)}, u32[]{:S(2)}) %copy-start.1) | copy-done | bytes 327704
  24.7 0.7 %copy-done.3 = f32[640,128]{1,0:T(8,128)} copy-done((f32[640,128]{1,0:T(8,128)}, f32[640,128]{1,0:T(8,128)S(1)}, u32[]{:S(2)}) %copy-start.3) | copy-done | bytes 327704
  25.5 2.1 %slice.101 = bf16[2,15,18,384]{3,2,1,0:T(8,128)(2,1)} slice(bf16[2,18,24,384]{3,2,1,0:T(8,128)(2,1)} %param.8), slice={[0:2], [3:18], [6:24], [0:384]} | slice | bytes 829440 | tf_op jit(solution)/shard_map/slice | solution.py:231
  27.6 0.9 %copy.49.reg_col = s32[4,144,1]{2,1,0:T(8,128)} copy(s32[4,144,1]{1,0,2:T(4,128)S(1)} %get-tuple-element.32) | data formatting | bytes 4608 | tf_op jit(solution)/shard_map/broadcast_in_dim | solution.py:206
  28.8 0.9 %slice.133 = bf16[2,3,18,384]{3,2,1,0:T(8,128)(2,1)S(1)} slice(bf16[2,3,24,384]{3,2,1,0:T(8,128)(2,1)} %collective-permute-done.1), slice={[0:2], [0:3], [6:24], [0:384]} | slice | bytes 165888 | tf_op jit(solution)/shard_map/slice | solution.py:232
  29.8 0.9 %slice.132 = bf16[2,15,6,384]{3,2,1,0:T(8,128)(2,1)S(1)} slice(bf16[2,18,6,384]{3,2,1,0:T(8,128)(2,1)} %collective-permute-done), slice={[0:2], [3:18], [0:6], [0:384]} | slice | bytes 276480 | tf_op jit(solution)/shard_map/slice | solution.py:231
  30.7 1.2 %maximum_maximum_fusion = bf16[2,18,24,384]{3,2,1,0:T(8,128)(2,1)S(1)} fusion(bf16[2,3,6,384]{3,2,1,0:T(8,128)(2,1)} %collective-permute-done.2, bf16[2,3,18,384]{3,2,1,0:T(8,128)(2,1)S(1)} %slice.133, bf16[2,15,6,384]{3,2,1,0:T(8,128)(2,1)S(1)} %slice.132, bf16[2,15,18,384]{3,2,1,0:T(8,128)(2,1)} %slice.101), kind=kLoop, calls=%fused_computation | loop fusion | flops 2654208 | bytes 1327104 | tf_op jit(solution)/shard_map/concatenate | solution.py:233
  32.1 0.5 copy.39
  32.6 0.5 copy.40
  33.3 0.6 %fusion.1 = (bf16[2,1,144,384]{3,1,2,0:T(2,128)(2,1)S(1)}, bf16[2,1,144,384]{3,1,2,0:T(2,128)(2,1)S(1)}) fusion(bf16[3,2,144,384]{3,1,2,0:T(2,128)(2,1)S(1)} %bitcast.40), kind=kLoop, calls=%fused_computation.15 | loop fusion | bytes 884736 | tf_op jit(solution)/shard_map/slice | solution.py:273
  34.6 0.7 %copy-done.5 = bf16[384,1536]{1,0:T(8,128)(2,1)S(1)} copy-done((bf16[384,1536]{1,0:T(8,128)(2,1)S(1)}, bf16[384,1536]{1,0:T(8,128)(2,1)}, u32[]{:S(2)}) %copy-start.5) | copy-done | bytes 1179672
  35.9 8.8 %layer.2 = bf16[4,144,384]{2,1,0:T(8,128)(2,1)S(1)} custom-call(bf16[4,144,384]{2,1,0:T(8,128)(2,1)S(1)} %pad_maximum_fusion.1.x, s32[4,1,144]{2,1,0:T(1,128)S(1)} %broadcast_in_dim.6.reg_row, s32[4,144,1]{2,1,0:T(8,128)S(1)} %copy-done.8, f32[5760,128]{1,0:T(8,128)S(1)} %get-tuple-element.8.refs_0_.refs_3_, f32[640,128]{1,0:T(8,128)S(1)} %copy-done.2, ...), custom_call_target="tpu_custom_call" | custom-call | flops 6115295232 | bytes 5603328 | tf_op jit(solution)/shard_map/layer/pallas_call | solution.py:186
  46.9 1.6 %collective-permute-start.5 = (bf16[2,15,6,384]{3,0,2,1:T(2,128)(2,1)S(1)}, bf16[2,15,6,384]{3,0,2,1:T(2,128)(2,1)S(1)}, u32[]{:S(2)}, u32[]{:S(2)}) collective-permute-start(bf16[2,15,6,384]{3,0,2,1:T(2,128)(2,1)S(1)} %pad_maximum_fusion.2), channel_id=1, source_target_pairs={{0,1},{1,2},{2,3},{3,0},{4,5},{5,6},{6,7},{7,4},{8,9},{9,10},{10,1... | collective-permute-start | bytes 414728 | tf_op jit(solution)/shard_map/ppermute | solution.py:212
  48.8 4.4 %layer.3 = bf16[2,144,384]{2,1,0:T(8,128)(2,1)S(1)} custom-call(bf16[2,144,384]{2,1,0:T(8,128)(2,1)S(1)} %get-tuple-element.34.x, s32[2,1,144]{2,1,0:T(1,128)S(1)} %get-tuple-element.30.reg_row, s32[2,144,1]{2,1,0:T(8,128)S(1)} %broadcast_in_dim_reshape.4.reg_col, f32[5760,128]{1,0:T(8,128)S(1)} %get-tuple-element.8.refs_0_.refs_3_, ...), custom_call_target="tpu_custom_call" | custom-call | flops 3057647616 | bytes 5160960 | tf_op jit(solution)/shard_map/layer/pallas_call | solution.py:186
  54.0 0.6 %collective-permute-done.5 = bf16[2,15,6,384]{3,0,2,1:T(2,128)(2,1)S(1)} collective-permute-done((bf16[2,15,6,384]{3,0,2,1:T(2,128)(2,1)S(1)}, bf16[2,15,6,384]{3,0,2,1:T(2,128)(2,1)S(1)}, u32[]{:S(2)}, u32[]{:S(2)}) %collective-permute-start.5) | collective-permute-done | bytes 138272 | tf_op jit(solution)/shard_map/ppermute | solution.py:212
  54.7 2.6 %maximum_maximum_fusion.1 = bf16[2,18,24,384]{3,0,2,1:T(2,128)(2,1)S(1)} fusion(bf16[2,3,18,384]{3,0,2,1:T(2,128)(2,1)S(1)} %get-tuple-element.20, bf16[2,12,6,384]{3,0,2,1:T(2,128)(2,1)S(1)} %get-tuple-element.22, bf16[2,12,12,384]{3,0,2,1:T(2,128)(2,1)S(1)} %bitcast.51, bf16[2,15,6,384]{3,0,2,1:T(2,128)(2,1)S(1)} %collective-permute-done.5, ...), kind=kLoop, calls=%fused_computation.2 | loop fusion | flops 1658880 | bytes 1327104 | tf_op jit(solution)/shard_map/concatenate | solution.py:282
  57.3 0.9 %copy.58 = bf16[2,18,24,384]{3,2,1,0:T(8,128)(2,1)} copy(bf16[2,18,24,384]{3,0,2,1:T(2,128)(2,1)S(1)} %maximum_maximum_fusion.1) | data formatting | bytes 1327104 | tf_op jit(solution)/shard_map/concatenate | solution.py:282
  (71 shorter events, 5.7 us)
Async XLA Ops:
  0.0 11.3 %copy-start.9 = (bf16[3,3312,12]{1,2,0:T(8,128)(2,1)S(1)}, bf16[3,3312,12]{1,2,0:T(8,128)(2,1)}, u32[]{:S(2)}) copy-start(bf16[3,3312,12]{1,2,0:T(8,128)(2,1)} %param.11) | copy-start | bytes 715396
  1.7 28.1 %collective-permute-start = (bf16[2,18,6,384]{3,2,1,0:T(8,128)(2,1)}, bf16[2,18,6,384]{3,2,1,0:T(8,128)(2,1)}, u32[]{:S(2)}, u32[]{:S(2)}) collective-permute-start(bf16[2,18,6,384]{3,2,1,0:T(8,128)(2,1)} %slice.102), channel_id=1, source_target_pairs={{0,3},{1,0},{2,1},{3,2},{4,7},{5,4},{6,5},{7,6},{8,11},{9,8},{10,9... | collective-permute-start | bytes 497672 | tf_op jit(solution)/shard_map/ppermute | solution.py:212
  8.3 20.5 %collective-permute-start.1 = (bf16[2,3,24,384]{3,2,1,0:T(8,128)(2,1)}, bf16[2,3,24,384]{3,2,1,0:T(8,128)(2,1)}, u32[]{:S(2)}, u32[]{:S(2)}) collective-permute-start(bf16[2,3,24,384]{3,2,1,0:T(8,128)(2,1)} %slice.104), channel_id=1, source_target_pairs={{0,4},{4,0},{1,5},{5,1},{2,6},{6,2},{3,7},{7,3},{8,12},{12,8},{9,1... | collective-permute-start | bytes 331784 | tf_op jit(solution)/shard_map/ppermute | solution.py:212
  9.7 21.0 %collective-permute-start.2 = (bf16[2,3,6,384]{3,2,1,0:T(8,128)(2,1)}, bf16[2,3,6,384]{3,2,1,0:T(8,128)(2,1)}, u32[]{:S(2)}, u32[]{:S(2)}) collective-permute-start(bf16[2,3,6,384]{3,2,1,0:T(8,128)(2,1)} %slice.106), channel_id=1, source_target_pairs={{0,7},{1,4},{2,5},{3,6},{4,3},{5,0},{6,1},{7,2},{8,15},{9,12},{10,... | collective-permute-start | bytes 82952 | tf_op jit(solution)/shard_map/ppermute | solution.py:222
  10.3 1.4 %slice-start.1 = ((s32[144,144]{1,0:T(8,128)}), s32[128,144]{1,0:T(8,128)S(1)}, s32[]{:S(2)}) async-start(s32[144,144]{1,0:T(8,128)} %param.10), calls=%async_computation.1 | async-start | bytes 262144 | tf_op jit(solution)/shard_map/slice | solution.py:82
  11.1 0.7 %slice-start.2 = ((s32[144,144]{1,0:T(8,128)}), s32[16,144]{1,0:T(8,128)S(1)}, s32[]{:S(2)}) async-start(s32[144,144]{1,0:T(8,128)} %param.10), calls=%async_computation.2 | async-start | bytes 32768 | tf_op jit(solution)/shard_map/slice | solution.py:83
  23.9 0.7 %copy-start.1 = (f32[640,128]{1,0:T(8,128)}, f32[640,128]{1,0:T(8,128)S(1)}, u32[]{:S(2)}) copy-start(f32[640,128]{1,0:T(8,128)S(1)} %get-tuple-element.9.refs_1_.refs_4_) | copy-start | bytes 983044
  24.7 0.7 %copy-start.3 = (f32[640,128]{1,0:T(8,128)}, f32[640,128]{1,0:T(8,128)S(1)}, u32[]{:S(2)}) copy-start(f32[640,128]{1,0:T(8,128)S(1)} %get-tuple-element.10.refs_2_.refs_5_) | copy-start | bytes 983044
  25.4 3.1 %slice-start = ((bf16[384,1152]{1,0:T(8,128)(2,1)}), bf16[384,384]{1,0:T(8,128)(2,1)S(1)}, s32[]{:S(2)}) async-start(bf16[384,1152]{1,0:T(8,128)(2,1)} %refs_6_.3), calls=%async_computation | async-start | bytes 589824 | tf_op jit(solution)/shard_map/slice | solution.py:250
  33.3 1.3 %copy-start.6 = (bf16[1536,384]{1,0:T(8,128)(2,1)S(1)}, bf16[1536,384]{1,0:T(8,128)(2,1)}, u32[]{:S(2)}) copy-start(bf16[1536,384]{1,0:T(8,128)(2,1)} %refs_10_.3) | copy-start | bytes 3538948
  33.3 1.3 %copy-start.8 = (s32[4,144,1]{2,1,0:T(8,128)S(1)}, s32[4,144,1]{2,1,0:T(8,128)}, u32[]{:S(2)}) copy-start(s32[4,144,1]{2,1,0:T(8,128)} %copy.49.reg_col) | copy-start | bytes 6916
  33.9 1.4 %copy-start.5 = (bf16[384,1536]{1,0:T(8,128)(2,1)S(1)}, bf16[384,1536]{1,0:T(8,128)(2,1)}, u32[]{:S(2)}) copy-start(bf16[384,1536]{1,0:T(8,128)(2,1)} %refs_9_.3) | copy-start | bytes 3538948
  34.1 1.5 %copy-start = (bf16[384,1152]{1,0:T(8,128)(2,1)S(1)}, bf16[384,1152]{1,0:T(8,128)(2,1)}, u32[]{:S(2)}) copy-start(bf16[384,1152]{1,0:T(8,128)(2,1)} %refs_6_.3) | copy-start | bytes 2654212
  34.1 1.5 %copy-start.2 = (f32[640,128]{1,0:T(8,128)S(1)}, f32[640,128]{1,0:T(8,128)}, u32[]{:S(2)}) copy-start(f32[640,128]{1,0:T(8,128)} %copy-done.1) | copy-start | bytes 983044
  34.2 1.6 %copy-start.4 = (f32[640,128]{1,0:T(8,128)S(1)}, f32[640,128]{1,0:T(8,128)}, u32[]{:S(2)}) copy-start(f32[640,128]{1,0:T(8,128)} %copy-done.3) | copy-start | bytes 983044
  34.2 1.7 %copy-start.7 = (bf16[384,384]{1,0:T(8,128)(2,1)S(1)}, bf16[384,384]{1,0:T(8,128)(2,1)}, u32[]{:S(2)}) copy-start(bf16[384,384]{1,0:T(8,128)(2,1)} %refs_8_.3) | copy-start | bytes 884740
  46.9 7.7 %collective-permute-start.5 = (bf16[2,15,6,384]{3,0,2,1:T(2,128)(2,1)S(1)}, bf16[2,15,6,384]{3,0,2,1:T(2,128)(2,1)S(1)}, u32[]{:S(2)}, u32[]{:S(2)}) collective-permute-start(bf16[2,15,6,384]{3,0,2,1:T(2,128)(2,1)S(1)} %pad_maximum_fusion.2), channel_id=1, source_target_pairs={{0,1},{1,2},{2,3},{3,0},{4,5},{5,6},{6,7},{7,4},{8,9},{9,10},{10,1... | collective-permute-start | bytes 414728 | tf_op jit(solution)/shard_map/ppermute | solution.py:212
  48.6 5.4 %collective-permute-start.4 = (bf16[2,3,18,384]{3,0,2,1:T(2,128)(2,1)S(1)}, bf16[2,3,18,384]{3,0,2,1:T(2,128)(2,1)S(1)}, u32[]{:S(2)}, u32[]{:S(2)}) collective-permute-start(bf16[2,3,18,384]{3,0,2,1:T(2,128)(2,1)S(1)} %get-tuple-element.19), channel_id=1, source_target_pairs={{0,4},{4,0},{1,5},{5,1},{2,6},{6,2},{3,7},{7,3},{8,12},{12,8},{9,1... | collective-permute-start | bytes 248840 | tf_op jit(solution)/shard_map/ppermute | solution.py:212
  48.6 5.4 %collective-permute-start.3 = (bf16[2,3,6,384]{3,0,2,1:T(2,128)(2,1)S(1)}, bf16[2,3,6,384]{3,0,2,1:T(2,128)(2,1)S(1)}, u32[]{:S(2)}, u32[]{:S(2)}) collective-permute-start(bf16[2,3,6,384]{3,0,2,1:T(2,128)(2,1)S(1)} %get-tuple-element.17), channel_id=1, source_target_pairs={{0,5},{1,6},{2,7},{3,4},{4,1},{5,2},{6,3},{7,0},{8,13},{9,14},{10,... | collective-permute-start | bytes 82952 | tf_op jit(solution)/shard_map/ppermute | solution.py:222

commit v3 on v2

v3 whole, which is shorter than its diff:
```python
import functools
import math

import jax
import jax.numpy as jnp
from jax import lax
from jax.experimental import pallas as pl
from jax.experimental.pallas import tpu as pltpu
from jax.sharding import PartitionSpec as P

WZ = 2
WLAT = 6
WLON = 12
EPS_NORM = 1e-05
LOG2E = math.log2(math.e)
LO = 256
LANES = 128
AT_ONCE = 4
GRANT = 32 * 1024 * 1024
NT = (((1,), (1,)), ((), ()))


def norm_rows(wide):
    average = jnp.mean(wide, axis=-1, keepdims=True)
    centred = wide - average
    spread = jnp.mean(centred * centred, axis=-1, keepdims=True)
    return (centred * lax.rsqrt(spread + EPS_NORM)).astype(jnp.bfloat16)


def bias_kernel(slab, with_rest, *refs):
    main_idx, rest_idx, table, main_out, rest_a, rest_b = refs if with_rest else (
        refs[0], None, refs[1], refs[2], None, None
    )
    tokens = main_idx.shape[0]
    pieces = table.shape[0] // slab
    low = lax.broadcasted_iota(jnp.int32, (LO, LANES), 0)

    def lookup(lines):
        spots = [jnp.where(low == (row & (LO - 1)), 1.0, 0.0).astype(jnp.bfloat16) for row in lines]
        found = jnp.dot(
            table[...], jnp.concatenate(spots, axis=1), preferred_element_type=jnp.float32
        )
        picked = []
        for place, row in enumerate(lines):
            high = row // LO
            columns = found[:, place * LANES : (place + 1) * LANES]
            total = columns[(pieces - 1) * slab :]
            for piece in range(pieces - 1):
                total = jnp.where(high == piece, columns[piece * slab : (piece + 1) * slab], total)
            picked.append(total * LOG2E)
        return picked

    @pl.loop(0, tokens // 8)
    def _(block):
        rows = main_idx[pl.ds(pl.multiple_of(block * 8, 8), 8), :]
        for start in range(0, 8, AT_ONCE):
            lines = [rows[start + line : start + line + 1] for line in range(AT_ONCE)]
            for line, values in enumerate(lookup(lines)):
                main_out[pl.ds(block * 8 + start + line, slab, stride=tokens), :] = values

    if not with_rest:
        return
    rest = rest_idx.shape[0]

    @pl.loop(0, rest // 8)
    def _(block):
        rows = rest_idx[pl.ds(pl.multiple_of(block * 8, 8), 8), :]
        for start in range(0, 8, AT_ONCE // 2):
            lines = []
            for line in range(start, start + AT_ONCE // 2):
                lines += [rows[line : line + 1, :LANES], rows[line : line + 1, LANES:]]
            for line, values in enumerate(lookup(lines)):
                target = rest_b if line % 2 else rest_a
                target[pl.ds(block * 8 + start + line // 2, slab, stride=rest), :] = values


def bias_tables(earth_bias, bias_index):
    bands, positions, heads = earth_bias.shape
    tokens = bias_index.shape[0]
    rest = tokens - LANES
    count = bands * heads
    slab = -(-count // 8) * 8
    pieces = -(-positions // LO)
    table = earth_bias.transpose(0, 2, 1).reshape(count, positions)
    table = jnp.pad(table, ((0, slab - count), (0, pieces * LO - positions)))
    table = table.reshape(slab, pieces, LO).transpose(1, 0, 2).reshape(pieces * slab, LO)
    main_idx = bias_index[:LANES].T
    rest_idx = jnp.pad(bias_index[LANES:], ((0, 0), (0, 2 * LANES - tokens)))
    half = tokens // 2
    main_shape = jax.ShapeDtypeStruct((slab * half, LANES), jnp.float32)
    rest_shape = jax.ShapeDtypeStruct((slab * rest, LANES), jnp.float32)

    def call(with_rest, shapes, *args):
        return pl.pallas_call(
            functools.partial(bias_kernel, slab, with_rest),
            out_shape=shapes,
            compiler_params=pltpu.CompilerParams(vmem_limit_bytes=GRANT // 2),
            cost_estimate=pl.CostEstimate(
                flops=table.size * tokens * tokens, bytes_accessed=slab * tokens * tokens * 2,
                transcendentals=0,
            ),
            name="bias_lookup",
        )(*args, table)

    first = call(False, main_shape, main_idx[:half])
    return first, lambda: call(True, (main_shape, rest_shape, rest_shape), main_idx[half:], rest_idx)


def attend_window(heads, normed, query, key, row, col, bias_first, bias_second, bias_a, bias_b, w_vt, turned):
    tokens, width = normed.shape
    dim = width // heads
    per = LANES // dim
    rest = tokens - LANES
    scale = dim ** (-0.5) * LOG2E
    value_t = lax.dot_general(w_vt[...], normed, NT, preferred_element_type=jnp.float32)
    value_t = value_t.astype(jnp.bfloat16)
    barred = jnp.where(col == row[:, :LANES], 0.0, -jnp.inf)
    owner = lax.broadcasted_iota(jnp.int32, (LANES, LANES), 1) // dim
    zero = jnp.zeros((), jnp.bfloat16)
    for group in range(width // LANES):
        span = slice(group * LANES, (group + 1) * LANES)
        asked = query[:LANES, span]
        stacked = jnp.concatenate([jnp.where(owner == h, asked, zero) for h in range(per)], axis=0)
        raw = lax.dot_general(key[:, span], stacked, NT, preferred_element_type=jnp.float32)
        for h in range(per):
            head = group * per + h
            scores = raw[:, h * LANES : (h + 1) * LANES] * scale
            span_of = slice(head * (tokens // 2), (head + 1) * (tokens // 2))
            bias = jnp.concatenate([bias_first[span_of, :], bias_second[span_of, :]], axis=0)
            scores = scores + bias + barred
            grown = jnp.exp2(scores - jnp.max(scores, axis=0, keepdims=True))
            total = jnp.sum(grown, axis=0, keepdims=True)
            mixed = jnp.dot(
                value_t[head * dim : (head + 1) * dim],
                grown.astype(jnp.bfloat16),
                preferred_element_type=jnp.float32,
            )
            turned[head * dim : (head + 1) * dim, :] = mixed / total
    owner = lax.broadcasted_iota(jnp.int32, (rest, width), 1) // dim
    asked = query[LANES:]
    stacked = jnp.concatenate([jnp.where(owner == h, asked, zero) for h in range(heads)], axis=0)
    scores = lax.dot_general(stacked, key, NT, preferred_element_type=jnp.float32) * scale
    scores = scores + jnp.concatenate([bias_a[...], bias_b[:, : tokens - LANES]], axis=1)
    barred = jnp.where(col[LANES:] == row, 0.0, -jnp.inf)
    scores = scores + jnp.concatenate([barred] * heads, axis=0)
    grown = jnp.exp2(scores - jnp.max(scores, axis=1, keepdims=True))
    total = jnp.sum(grown, axis=1, keepdims=True)
    mixed = lax.dot_general(
        grown.astype(jnp.bfloat16), value_t, NT, preferred_element_type=jnp.float32
    )
    mixed = mixed / total
    last = jnp.zeros((rest, width), jnp.float32)
    for h in range(heads):
        last = jnp.where(owner == h, mixed[h * rest : (h + 1) * rest], last)
    return jnp.concatenate([turned[...].T, last], axis=0).astype(jnp.bfloat16)


def layer_kernel(heads, together, x, reg_row, reg_col, *refs):
    biases, (w_qkv, w_vt, w_proj, w_fc1, w_fc2, out, turned) = refs[: 4 * together], refs[4 * together :]
    tokens, width = x.shape[1:]
    fields = x[...].reshape(together * tokens, width)
    normed = norm_rows(fields)
    packed = jnp.dot(normed, w_qkv[:, : 2 * width], preferred_element_type=jnp.float32)
    packed = packed.astype(jnp.bfloat16)
    contexts = []
    for place in range(together):
        rows = slice(place * tokens, (place + 1) * tokens)
        contexts.append(
            attend_window(
                heads, normed[rows], packed[rows, :width], packed[rows, width:], reg_row[place],
                reg_col[place], *biases[4 * place : 4 * place + 4], w_vt, turned.at[place],
            )
        )
    context = jnp.concatenate(contexts, axis=0)
    projected = jnp.dot(context, w_proj[...], preferred_element_type=jnp.float32)
    projected = projected.astype(jnp.bfloat16).astype(jnp.float32)
    residual = (fields + projected).astype(jnp.bfloat16).astype(jnp.float32)
    normed = norm_rows(residual)
    grown = jnp.dot(normed, w_fc1[...], preferred_element_type=jnp.float32)
    hidden = (0.5 * grown * (1.0 + lax.erf(grown * math.sqrt(0.5)))).astype(jnp.bfloat16)
    summed = residual + jnp.dot(hidden, w_fc2[...], preferred_element_type=jnp.float32)
    out[...] = summed.reshape(out.shape)


def layer(windows, regions, tables, band_of, heads, w_qkv, w_vt, w_proj, w_fc1, w_fc2):
    count, tokens, width = windows.shape
    rest = tokens - LANES
    together = 2 if count % 2 == 0 else 1
    whole = lambda w: (0, 0)
    bias_specs, bias_args = [], []
    for place in range(together):
        band = lambda w, place=place: (band_of(w * together + place), 0)
        for table, rows in zip(tables, (tokens // 2, tokens // 2, rest, rest)):
            bias_specs.append(pl.BlockSpec((heads * rows, LANES), band))
            bias_args.append(table)
    weights = (w_qkv, w_vt, w_proj, w_fc1, w_fc2)
    return pl.pallas_call(
        functools.partial(layer_kernel, heads, together),
        grid=(count // together,),
        out_shape=jax.ShapeDtypeStruct(windows.shape, jnp.float32),
        in_specs=[
            pl.BlockSpec((together, tokens, width), lambda w: (w, 0, 0)),
            pl.BlockSpec((together, 1, tokens), lambda w: (w, 0, 0)),
            pl.BlockSpec((together, tokens, 1), lambda w: (w, 0, 0)),
            *bias_specs,
            *[pl.BlockSpec(weight.shape, whole) for weight in weights],
        ],
        out_specs=pl.BlockSpec((together, tokens, width), lambda w: (w, 0, 0)),
        scratch_shapes=[pltpu.VMEM((together, width, LANES), jnp.float32)],
        compiler_params=pltpu.CompilerParams(vmem_limit_bytes=GRANT),
        cost_estimate=pl.CostEstimate(
            flops=2 * count * tokens * (w_qkv.size + w_proj.size + w_fc1.size + w_fc2.size) * 3,
            bytes_accessed=windows.size * 4 + w_fc1.size * 8,
            transcendentals=count * heads * tokens * tokens,
        ),
        name="layer",
    )(windows, regions[:, None, :], regions[:, :, None], *bias_args, *weights)


def from_behind(value, axis, steps):
    count = lax.axis_size(axis)
    pairs = [(source, (source + steps) % count) for source in range(count)]
    return lax.ppermute(value, axis, pairs)


def from_corner(value, steps):
    lats, lons = lax.axis_size("lat"), lax.axis_size("lon")
    pairs = [
        (a * lons + o, (a + steps) % lats * lons + (o + steps) % lons)
        for a in range(lats)
        for o in range(lons)
    ]
    return lax.ppermute(value, ("lat", "lon"), pairs)


def pack_kernel(fields, cols, rows, corner):
    half_lat = rows.shape[1]
    lons = cols.shape[2]
    cols[...] = fields[:, half_lat:, :lons, :]
    rows[...] = fields[:, :half_lat]
    corner[...] = fields[:, :half_lat, :lons, :]


def window_slot(lat_wins, lon_wins, t, b):
    if t == lat_wins - 1:
        return 0, lat_wins - 1 + b
    if b == lon_wins - 1:
        return 0, t
    return 1, t * (lon_wins - 1) + b


def spread_kernel(fields, cols, rows, corner, *outs):
    levels, lat_rows, lon_cols, width = fields.shape
    half_lat, half_lon = WLAT // 2, WLON // 2
    lat_wins, lon_wins = lat_rows // WLAT, lon_cols // WLON
    for level in range(levels):
        source = (level + WZ // 2) % levels
        for a in range(lat_rows):
            away = a - (lat_rows - half_lat)
            own = fields[source, a + half_lat] if away < 0 else rows[source, away]
            halo = cols[source, a] if away < 0 else corner[source, away]
            line = [own.astype(jnp.float32)[half_lon:], halo.astype(jnp.float32)[:half_lon]]
            line = jnp.concatenate(line, axis=0)
            place = (level * WLAT + a % WLAT) * WLON
            for b in range(lon_wins):
                which, slot = window_slot(lat_wins, lon_wins, a // WLAT, b)
                outs[which][slot, place : place + WLON, :] = line[b * WLON : (b + 1) * WLON]


def window_row(wins, lat_wins, lon_wins, level, a):
    place = (level * WLAT + a % WLAT) * WLON
    parts = []
    for b in range(lon_wins):
        which, slot = window_slot(lat_wins, lon_wins, a // WLAT, b)
        parts.append(wins[which][slot, place : place + WLON, :])
    return parts


def back_kernel(lat_wins, lon_wins, edge, cols, rows, corner):
    levels, upper, spare = cols.shape[:3]
    half_lon = WLON // 2
    for level in range(levels):
        target = (level + WZ // 2) % levels
        for a in range(lat_wins * WLAT):
            which, slot = window_slot(lat_wins, lon_wins, a // WLAT, lon_wins - 1)
            place = (level * WLAT + a % WLAT) * WLON
            last = edge[slot, place : place + WLON, :]
            sent = jnp.concatenate([last[half_lon:], last[: spare - half_lon]], axis=0)
            if a < upper:
                cols[target, a] = sent.astype(jnp.bfloat16)
            else:
                corner[target, a - upper] = sent.astype(jnp.bfloat16)
                line = window_row((edge,), lat_wins, lon_wins, level, a)
                rows[target, a - upper] = jnp.concatenate(line, axis=0).astype(jnp.bfloat16)


def join_kernel(*refs):
    wins, (cols, rows, corner, out) = refs[:-4], refs[-4:]
    levels, lat_rows, lon_cols, width = out.shape
    half_lat, half_lon = WLAT // 2, WLON // 2
    lat_wins, lon_wins = lat_rows // WLAT, lon_cols // WLON
    for level in range(levels):
        target = (level + WZ // 2) % levels
        for a in range(-half_lat, lat_rows - half_lat):
            if a < 0:
                halo = corner[target, a + half_lat].astype(jnp.float32)
                kept = rows[target, a + half_lat].astype(jnp.float32)
            else:
                halo = cols[target, a].astype(jnp.float32)
                kept = jnp.concatenate(window_row(wins, lat_wins, lon_wins, level, a), axis=0)
            line = jnp.concatenate([halo[:half_lon], kept[: lon_cols - half_lon]], axis=0)
            out[target, a + half_lat] = line.astype(jnp.bfloat16)


def small(kernel, shapes, name, *args):
    size = sum(arg.size for arg in args)
    return pl.pallas_call(
        kernel,
        out_shape=shapes,
        compiler_params=pltpu.CompilerParams(vmem_limit_bytes=GRANT // 2),
        cost_estimate=pl.CostEstimate(flops=size, bytes_accessed=4 * size, transcendentals=0),
        name=name,
    )(*args)


def local(fields, region_ids, bias_index, earth_bias, w_qkv, w_proj, w_fc1, w_fc2):
    levels, lat_rows, lon_cols, width = fields.shape
    lat_wins = lat_rows // WLAT
    lon_wins = lon_cols // WLON
    tokens = levels * WLAT * WLON
    half_lat = WLAT // 2
    heads = earth_bias.shape[-1]
    spare = -(-(WLON // 2) // 8) * 8
    halo_shapes = tuple(
        jax.ShapeDtypeStruct((levels, lats, lons, width), jnp.bfloat16)
        for lats, lons in ((lat_rows - half_lat, spare), (half_lat, lon_cols), (half_lat, spare))
    )
    first, second_call = bias_tables(earth_bias, bias_index)
    halos = small(pack_kernel, halo_shapes, "pack", fields)
    first, *halos = lax.optimization_barrier((first, *halos))
    cols = from_behind(halos[0], "lon", -1)
    rows = from_behind(halos[1], "lat", -1)
    corner = from_corner(halos[2], -1)
    tables = (first, *second_call())
    regions = region_ids.reshape(levels, lat_wins, WLAT, lon_wins, WLON)
    regions = regions.transpose(1, 3, 0, 2, 4).reshape(lat_wins, lon_wins, tokens)
    counts = [lat_wins - 1 + lon_wins, (lat_wins - 1) * (lon_wins - 1)]
    window_shapes = tuple(
        jax.ShapeDtypeStruct((count, tokens, width), jnp.float32) for count in counts if count
    )
    windows = small(spread_kernel, window_shapes, "spread", fields, cols, rows, corner)
    weights = (w_qkv, w_qkv[:, 2 * width :].T, w_proj, w_fc1, w_fc2)
    edge_regions = jnp.concatenate([regions[:-1, -1], regions[-1]], axis=0)
    results = [
        layer(
            windows[0], edge_regions, tables,
            lambda w: jnp.minimum(w, lat_wins - 1), heads, *weights,
        )
    ]
    halos = small(
        functools.partial(back_kernel, lat_wins, lon_wins), halo_shapes, "pack_back", results[0]
    )
    cols = from_behind(halos[0], "lon", 1)
    rows = from_behind(halos[1], "lat", 1)
    corner = from_corner(halos[2], 1)
    if len(windows) > 1:
        inner_regions = regions[:-1, :-1].reshape(-1, tokens)
        results.append(
            layer(
                windows[1], inner_regions, tables,
                lambda w: w // (lon_wins - 1), heads, *weights,
            )
        )
    shape = jax.ShapeDtypeStruct(fields.shape, jnp.bfloat16)
    return small(join_kernel, shape, "join", *results, cols, rows, corner)


def solution(mesh):
    return jax.shard_map(
        local,
        mesh=mesh,
        in_specs=(
            P("ens", "lat", "lon", None),
            P(None, "lat", "lon"),
            P(),
            P("lat", None, None),
            P(),
            P(),
            P(),
            P(),
        ),
        out_specs=P("ens", "lat", "lon", None),
        check_vma=False,
    )
```

time: 58.6 us -> 53.9 us (0.920)
  other arithmetic: 5.12 us -> 0.01 us
  local copies, waits for them, and re-layouts: 19.3 us -> 15 us
  Pallas kernels: 25.3 us -> 28.1 us
  waiting for transfers between devices: 0.64 us -> 2.55 us
    slice x21 -> x3, local copies, waits for them, and re-layouts: 10.8 us -> 1.34 us  [the longest x1 0.72 us: local(): edge_regions = jnp.concatenate([regions[:-1, -1], regions[-1]], axis=0)]
    unnamed x23 -> x37, local copies, waits for them, and re-layouts: 3.27 us -> 10.9 us
    concatenate x5 -> x0, other arithmetic: 4.18 us -> none  [the longest x1 2.65 us: local(): jnp.concatenate([jnp.concatenate([corner, rows], axis=2), own], axis=1)]
    pallas_call x1 -> x6, Pallas kernels: 12.1 us -> 14.8 us  [the longest x2 11.8 us: call(): pl.pallas_call(functools.partial(bias_kernel, slab, with_rest), out_shape...]
    ppermute x2, waiting for transfers between devices: 0.01 us -> 1.98 us  [from_corner(): return lax.ppermute(value, ('lat', 'lon'), pairs)]
    concatenate x2 -> x0, local copies, waits for them, and re-layouts: 1.44 us -> none  [the longest x1 0.92 us: local(): jnp.concatenate([jnp.concatenate([corner, rows], axis=2), own], axis=1)]
    reshape x1, local copies, waits for them, and re-layouts: 0.09 us -> 1.13 us  [bias_tables(): table = earth_bias.transpose(0, 2, 1).reshape(count, positions)]
    transpose x4 -> x0, local copies, waits for them, and re-layouts: 1.03 us -> none  [the longest x3 0.52 us: placed(): block.transpose(2, 0, 3, 1, 4, 5)]
  transfers between devices with their start and end apart: 6 -> 6, of which waited for: 1 -> 2; matrix products, arithmetic and copies ran while one was open for 18% -> 5% of each run, Pallas kernels for 28% -> 21%
where the time goes in v3:
time: 53.9 us; the launch traced here: 53.4 us
  Pallas kernels  28.1 us (52%)
  local copies, waits for them, and re-layouts  15 us (28%)
  starting transfers between devices  7.52 us (14%)
  waiting for transfers between devices  2.55 us (5%)
    pallas_call x2, Pallas kernels, layer(): pl.pallas_call(functools.partial(layer_kernel, heads, together), grid=(co...  13.2 us
    pallas_call x2, Pallas kernels, call(): pl.pallas_call(functools.partial(bias_kernel, slab, with_rest), out_shape...  11.8 us
    unnamed x37, local copies, waits for them, and re-layouts  10.9 us
    ppermute x4, starting transfers between devices, from_behind(): return lax.ppermute(value, axis, pairs)  6.77 us
    pallas_call x4, Pallas kernels, small(): pl.pallas_call(kernel, out_shape=shapes, compiler_params=pltpu.CompilerPa...  3.05 us
    ppermute x2, waiting for transfers between devices, from_corner(): return lax.ppermute(value, ('lat', 'lon'), pairs)  1.98 us
    reshape x1, local copies, waits for them, and re-layouts, bias_tables(): table = earth_bias.transpose(0, 2, 1).reshape(count, positions)  1.13 us
  transfers between devices with their start and end apart: 6, of which 2 were waited for; matrix products, arithmetic and copies ran while one was open for 5% of the time, Pallas kernels for 21%

profile of v3, /device:TPU:0, one launch (start us, length us, event | category | flops | bytes accessed | tf_op | source)
XLA Modules:
  0.0 53.4 jit_solution(3815756318384280400)
XLA Ops:
  0.0 1.1 %reshape.17 = bf16[36,3312]{1,0:T(8,128)(2,1)S(1)} reshape(bf16[3,12,3312]{2,1,0:T(8,128)(2,1)} %bitcast.20) | data formatting | bytes 476928 | tf_op jit(solution)/shard_map/reshape | solution.py:84
  1.6 0.8 %pack.1 = (bf16[2,15,8,384]{3,2,1,0:T(8,128)(2,1)}, bf16[2,3,24,384]{3,2,1,0:T(8,128)(2,1)}, bf16[2,3,8,384]{3,2,1,0:T(8,128)(2,1)}) custom-call(bf16[2,18,24,384]{3,2,1,0:T(8,128)(2,1)S(1)} %copy-done), custom_call_target="tpu_custom_call" | custom-call | flops 331776 | bytes 1327104 | tf_op jit(solution)/shard_map/pack/pallas_call | solution.py:317
  2.4 4.9 %bias_lookup.2.refs_0_.refs_4_ = f32[2880,128]{1,0:T(8,128)S(1)} custom-call(s32[72,128]{1,0:T(8,128)S(1)} %get-tuple-element.36.refs_0_, bf16[520,256]{1,0:T(8,128)(2,1)S(1)} %bitcast.17), custom_call_target="tpu_custom_call" | custom-call | flops 2760376320 | bytes 1658880 | tf_op jit(solution)/shard_map/bias_lookup/pallas_call | solution.py:94
  7.3 5.1 %collective-permute-start = (bf16[2,15,8,384]{3,2,1,0:T(8,128)(2,1)}, bf16[2,15,8,384]{3,2,1,0:T(8,128)(2,1)}, u32[]{:S(2)}, u32[]{:S(2)}) collective-permute-start(bf16[2,15,8,384]{3,2,1,0:T(8,128)(2,1)} %get-tuple-element.23), channel_id=1, source_target_pairs={{0,3},{1,0},{2,1},{3,2},{4,7},{5,4},{6,5},{7,6},{8,11},{9,8},{10,9... | collective-permute-start | bytes 552968 | tf_op jit(solution)/shard_map/ppermute | solution.py:223
  13.8 6.9 %bias_lookup.3 = (f32[2880,128]{1,0:T(8,128)S(1)}, f32[640,128]{1,0:T(8,128)S(1)}, f32[640,128]{1,0:T(8,128)S(1)}) custom-call(s32[72,128]{1,0:T(8,128)S(1)} %get-tuple-element.35.refs_0_, s32[16,256]{1,0:T(8,128)S(1)} %pad.9.refs_1_, bf16[520,256]{1,0:T(8,128)(2,1)S(1)} %bitcast.18), custom_call_target="tpu_custom_call" | custom-call | flops 2760376320 | bytes 1658880 | tf_op jit(solution)/shard_map/bias_lookup/pallas_call | solution.py:94
  20.6 0.7 %copy-done.4 = f32[640,128]{1,0:T(8,128)} copy-done((f32[640,128]{1,0:T(8,128)}, f32[640,128]{1,0:T(8,128)S(1)}, u32[]{:S(2)}) %copy-start.4) | copy-done | bytes 327704
  21.4 0.7 %copy-done.6 = f32[640,128]{1,0:T(8,128)} copy-done((f32[640,128]{1,0:T(8,128)}, f32[640,128]{1,0:T(8,128)S(1)}, u32[]{:S(2)}) %copy-start.6) | copy-done | bytes 327704
  22.1 0.6 %slice_reduce_fusion = (s32[2,144]{1,0:T(2,128)}, s32[2,1,144]{2,1,0:T(1,128)S(1)}, s32[2,1,144]{2,1,0:T(1,128)S(1)}) fusion(s32[3,2,144]{2,1,0:T(2,128)S(1)} %reshape.21), kind=kLoop, calls=%fused_computation.3 | loop fusion | bytes 5760 | tf_op jit(solution)/shard_map/slice | solution.py:367
  22.7 0.7 %slice.35 = s32[1,2,2,6,12]{4,3,2,1,0:T(8,128)S(1)} slice(s32[3,2,2,6,12]{4,3,2,1,0:T(8,128)} %bitcast.23), slice={[2:3], [0:2], [0:2], [0:6], [0:12]} | slice | bytes 2304 | tf_op jit(solution)/shard_map/slice | solution.py:353
  23.5 0.9 %copy.27.reg_col = s32[4,144,1]{2,1,0:T(8,128)} copy(s32[4,144,1]{1,0,2:T(4,128)S(1)} %get-tuple-element.40) | data formatting | bytes 4608 | tf_op jit(solution)/shard_map/broadcast_in_dim | solution.py:217
  24.7 1.1 %copy-done.1 = bf16[2,18,24,384]{3,2,1,0:T(8,128)(2,1)S(1)} copy-done((bf16[2,18,24,384]{3,2,1,0:T(8,128)(2,1)S(1)}, bf16[2,18,24,384]{3,2,1,0:T(8,128)(2,1)}, u32[]{:S(2)}) %copy-start.1) | copy-done | bytes 663576
  25.7 1.2 %spread.1 = (f32[4,144,384]{2,1,0:T(8,128)S(1)}, f32[2,144,384]{2,1,0:T(8,128)S(1)}) custom-call(bf16[2,18,24,384]{3,2,1,0:T(8,128)(2,1)S(1)} %copy-done.1, bf16[2,15,8,384]{3,2,1,0:T(8,128)(2,1)} %collective-permute-done.cols, bf16[2,3,24,384]{3,2,1,0:T(8,128)(2,1)} %collective-permute-done.1.rows, bf16[2,3,8,384]{3,2,1,0:T(8,128)(2,1)} %collective-permute-done.2.corner), custom_call_target="tpu_custom_call" | custom-call | flops 497664 | bytes 1990656 | tf_op jit(solution)/shard_map/spread/pallas_call | solution.py:317
  26.9 1.2 %copy-done.2 = bf16[384,1152]{1,0:T(8,128)(2,1)S(1)} copy-done((bf16[384,1152]{1,0:T(8,128)(2,1)S(1)}, bf16[384,1152]{1,0:T(8,128)(2,1)}, u32[]{:S(2)}) %copy-start.2) | copy-done | bytes 884760
  28.1 1.0 %copy-done.5 = f32[640,128]{1,0:T(8,128)S(1)} copy-done((f32[640,128]{1,0:T(8,128)S(1)}, f32[640,128]{1,0:T(8,128)}, u32[]{:S(2)}) %copy-start.5) | copy-done | bytes 327704
  29.1 1.0 %copy-done.7 = f32[640,128]{1,0:T(8,128)S(1)} copy-done((f32[640,128]{1,0:T(8,128)S(1)}, f32[640,128]{1,0:T(8,128)}, u32[]{:S(2)}) %copy-start.7) | copy-done | bytes 327704
  30.0 1.3 %copy-done.8 = bf16[384,1536]{1,0:T(8,128)(2,1)S(1)} copy-done((bf16[384,1536]{1,0:T(8,128)(2,1)S(1)}, bf16[384,1536]{1,0:T(8,128)(2,1)}, u32[]{:S(2)}) %copy-start.8) | copy-done | bytes 1179672
  31.3 1.3 %copy-done.10 = bf16[1536,384]{1,0:T(8,128)(2,1)S(1)} copy-done((bf16[1536,384]{1,0:T(8,128)(2,1)S(1)}, bf16[1536,384]{1,0:T(8,128)(2,1)}, u32[]{:S(2)}) %copy-start.10) | copy-done | bytes 1179672
  32.6 1.0 %copy-done.12 = bf16[384,384]{1,0:T(8,128)(2,1)S(1)} copy-done((bf16[384,384]{1,0:T(8,128)(2,1)S(1)}, bf16[384,384]{1,0:T(8,128)(2,1)}, u32[]{:S(2)}) %copy-start.12) | copy-done | bytes 294936
  33.5 1.0 %copy-done.13 = s32[4,144,1]{2,1,0:T(8,128)S(1)} copy-done((s32[4,144,1]{2,1,0:T(8,128)S(1)}, s32[4,144,1]{2,1,0:T(8,128)}, u32[]{:S(2)}) %copy-start.13) | copy-done | bytes 2328
  34.5 8.8 %layer.2.edge.refs_0_ = f32[4,144,384]{2,1,0:T(8,128)S(1)} custom-call(f32[4,144,384]{2,1,0:T(8,128)S(1)} %get-tuple-element.26.x, s32[4,1,144]{2,1,0:T(1,128)S(1)} %broadcast_in_dim.6.reg_row, s32[4,144,1]{2,1,0:T(8,128)S(1)} %copy-done.13, f32[2880,128]{1,0:T(8,128)S(1)} %bias_lookup.2.refs_0_.refs_4_, f32[2880,128]{1,0:T(8,128)S(1)} %get-tuple-element.28.refs_1_.refs_5_, ...), custom_call_target="tpu_custom_call" | custom-call | flops 6115295232 | bytes 5603328 | tf_op jit(solution)/shard_map/layer/pallas_call | solution.py:197
  43.6 1.6 %collective-permute-start.3 = (bf16[2,15,8,384]{3,2,1,0:T(8,128)(2,1)S(1)}, bf16[2,15,8,384]{3,2,1,0:T(8,128)(2,1)S(1)}, u32[]{:S(2)}, u32[]{:S(2)}) collective-permute-start(bf16[2,15,8,384]{3,2,1,0:T(8,128)(2,1)S(1)} %get-tuple-element.32), channel_id=1, source_target_pairs={{0,1},{1,2},{2,3},{3,0},{4,5},{5,6},{6,7},{7,4},{8,9},{9,10},{10,1... | collective-permute-start | bytes 552968 | tf_op jit(solution)/shard_map/ppermute | solution.py:223
  45.4 4.4 %layer.3.refs_1_ = f32[2,144,384]{2,1,0:T(8,128)S(1)} custom-call(f32[2,144,384]{2,1,0:T(8,128)S(1)} %get-tuple-element.31.x, s32[2,1,144]{2,1,0:T(1,128)S(1)} %get-tuple-element.38.reg_row, s32[2,144,1]{2,1,0:T(8,128)S(1)} %broadcast_in_dim_reshape.4.reg_col, f32[2880,128]{1,0:T(8,128)S(1)} %bias_lookup.2.refs_0_.refs_4_, ...), custom_call_target="tpu_custom_call" | custom-call | flops 3057647616 | bytes 5160960 | tf_op jit(solution)/shard_map/layer/pallas_call | solution.py:197
  49.8 2.0 %collective-permute-done.5.refs_4_ = bf16[2,3,8,384]{3,2,1,0:T(8,128)(2,1)S(1)} collective-permute-done((bf16[2,3,8,384]{3,2,1,0:T(8,128)(2,1)S(1)}, bf16[2,3,8,384]{3,2,1,0:T(8,128)(2,1)S(1)}, u32[]{:S(2)}, u32[]{:S(2)}) %collective-permute-start.5) | collective-permute-done | bytes 36896 | tf_op jit(solution)/shard_map/ppermute | solution.py:233
  52.4 1.0 %join.1 = bf16[2,18,24,384]{3,2,1,0:T(8,128)(2,1)} custom-call(f32[4,144,384]{2,1,0:T(8,128)S(1)} %layer.2.edge.refs_0_, f32[2,144,384]{2,1,0:T(8,128)S(1)} %layer.3.refs_1_, bf16[2,15,8,384]{3,2,1,0:T(8,128)(2,1)S(1)} %collective-permute-done.3.refs_2_, bf16[2,3,24,384]{3,2,1,0:T(8,128)(2,1)S(1)} %collective-permute-done.4.refs_3_, ...), custom_call_target="tpu_custom_call" | custom-call | flops 497664 | bytes 1990656 | tf_op jit(solution)/shard_map/join/pallas_call | solution.py:317
  (55 shorter events, 3.0 us)
Async XLA Ops:
  0.0 1.5 %slice-start.1 = ((s32[144,144]{1,0:T(8,128)}), s32[128,144]{1,0:T(8,128)S(1)}, s32[]{:S(2)}) async-start(s32[144,144]{1,0:T(8,128)} %param.10), calls=%async_computation.1 | async-start | bytes 262144 | tf_op jit(solution)/shard_map/slice | solution.py:87
  0.0 1.6 %copy-start = (bf16[2,18,24,384]{3,2,1,0:T(8,128)(2,1)S(1)}, bf16[2,18,24,384]{3,2,1,0:T(8,128)(2,1)}, u32[]{:S(2)}) copy-start(bf16[2,18,24,384]{3,2,1,0:T(8,128)(2,1)} %fields.3) | copy-start | bytes 1990660
  2.4 10.7 %copy-start.15 = (s32[2,18,24]{2,0,1:T(2,128)S(1)}, s32[2,18,24]{2,0,1:T(2,128)}, u32[]{:S(2)}) copy-start(s32[2,18,24]{2,0,1:T(2,128)} %param.9) | copy-start | bytes 10372
  2.4 10.9 %slice-start.2 = ((s32[144,144]{1,0:T(8,128)}), s32[16,144]{1,0:T(8,128)S(1)}, s32[]{:S(2)}) async-start(s32[144,144]{1,0:T(8,128)} %param.10), calls=%async_computation.2 | async-start | bytes 32768 | tf_op jit(solution)/shard_map/slice | solution.py:88
  7.3 17.3 %collective-permute-start = (bf16[2,15,8,384]{3,2,1,0:T(8,128)(2,1)}, bf16[2,15,8,384]{3,2,1,0:T(8,128)(2,1)}, u32[]{:S(2)}, u32[]{:S(2)}) collective-permute-start(bf16[2,15,8,384]{3,2,1,0:T(8,128)(2,1)} %get-tuple-element.23), channel_id=1, source_target_pairs={{0,3},{1,0},{2,1},{3,2},{4,7},{5,4},{6,5},{7,6},{8,11},{9,8},{10,9... | collective-permute-start | bytes 552968 | tf_op jit(solution)/shard_map/ppermute | solution.py:223
  12.5 12.2 %collective-permute-start.1 = (bf16[2,3,24,384]{3,2,1,0:T(8,128)(2,1)}, bf16[2,3,24,384]{3,2,1,0:T(8,128)(2,1)}, u32[]{:S(2)}, u32[]{:S(2)}) collective-permute-start(bf16[2,3,24,384]{3,2,1,0:T(8,128)(2,1)} %get-tuple-element.24), channel_id=1, source_target_pairs={{0,4},{4,0},{1,5},{5,1},{2,6},{6,2},{3,7},{7,3},{8,12},{12,8},{9,1... | collective-permute-start | bytes 331784 | tf_op jit(solution)/shard_map/ppermute | solution.py:223
  12.5 12.2 %collective-permute-start.2 = (bf16[2,3,8,384]{3,2,1,0:T(8,128)(2,1)}, bf16[2,3,8,384]{3,2,1,0:T(8,128)(2,1)}, u32[]{:S(2)}, u32[]{:S(2)}) collective-permute-start(bf16[2,3,8,384]{3,2,1,0:T(8,128)(2,1)} %get-tuple-element.25), channel_id=1, source_target_pairs={{0,7},{1,4},{2,5},{3,6},{4,3},{5,0},{6,1},{7,2},{8,15},{9,12},{10,... | collective-permute-start | bytes 110600 | tf_op jit(solution)/shard_map/ppermute | solution.py:233
  13.8 10.6 %slice-start = ((bf16[384,1152]{1,0:T(8,128)(2,1)}), bf16[384,384]{1,0:T(8,128)(2,1)S(1)}, s32[]{:S(2)}) async-start(bf16[384,1152]{1,0:T(8,128)(2,1)} %refs_8_.3), calls=%async_computation | async-start | bytes 589824 | tf_op jit(solution)/shard_map/slice | solution.py:352
  20.6 0.7 %copy-start.4 = (f32[640,128]{1,0:T(8,128)}, f32[640,128]{1,0:T(8,128)S(1)}, u32[]{:S(2)}) copy-start(f32[640,128]{1,0:T(8,128)S(1)} %get-tuple-element.29.refs_2_.refs_6_) | copy-start | bytes 983044
  24.6 1.1 %copy-start.1 = (bf16[2,18,24,384]{3,2,1,0:T(8,128)(2,1)S(1)}, bf16[2,18,24,384]{3,2,1,0:T(8,128)(2,1)}, u32[]{:S(2)}) copy-start(bf16[2,18,24,384]{3,2,1,0:T(8,128)(2,1)} %fields.3) | copy-start | bytes 1990660
  26.9 1.2 %copy-start.2 = (bf16[384,1152]{1,0:T(8,128)(2,1)S(1)}, bf16[384,1152]{1,0:T(8,128)(2,1)}, u32[]{:S(2)}) copy-start(bf16[384,1152]{1,0:T(8,128)(2,1)} %refs_8_.3) | copy-start | bytes 2654212
  28.1 1.0 %copy-start.5 = (f32[640,128]{1,0:T(8,128)S(1)}, f32[640,128]{1,0:T(8,128)}, u32[]{:S(2)}) copy-start(f32[640,128]{1,0:T(8,128)} %copy-done.4) | copy-start | bytes 983044
  29.1 1.0 %copy-start.7 = (f32[640,128]{1,0:T(8,128)S(1)}, f32[640,128]{1,0:T(8,128)}, u32[]{:S(2)}) copy-start(f32[640,128]{1,0:T(8,128)} %copy-done.6) | copy-start | bytes 983044
  30.0 1.3 %copy-start.8 = (bf16[384,1536]{1,0:T(8,128)(2,1)S(1)}, bf16[384,1536]{1,0:T(8,128)(2,1)}, u32[]{:S(2)}) copy-start(bf16[384,1536]{1,0:T(8,128)(2,1)} %refs_11_.3) | copy-start | bytes 3538948
  31.3 1.3 %copy-start.10 = (bf16[1536,384]{1,0:T(8,128)(2,1)S(1)}, bf16[1536,384]{1,0:T(8,128)(2,1)}, u32[]{:S(2)}) copy-start(bf16[1536,384]{1,0:T(8,128)(2,1)} %refs_12_.3) | copy-start | bytes 3538948
  32.6 1.0 %copy-start.12 = (bf16[384,384]{1,0:T(8,128)(2,1)S(1)}, bf16[384,384]{1,0:T(8,128)(2,1)}, u32[]{:S(2)}) copy-start(bf16[384,384]{1,0:T(8,128)(2,1)} %refs_10_.3) | copy-start | bytes 884740
  33.5 1.0 %copy-start.13 = (s32[4,144,1]{2,1,0:T(8,128)S(1)}, s32[4,144,1]{2,1,0:T(8,128)}, u32[]{:S(2)}) copy-start(s32[4,144,1]{2,1,0:T(8,128)} %copy.27.reg_col) | copy-start | bytes 6916
  34.5 8.9 %copy-start.16 = (s32[2,144]{1,0:T(2,128)S(1)}, s32[2,144]{1,0:T(2,128)}, u32[]{:S(2)}) copy-start(s32[2,144]{1,0:T(2,128)} %get-tuple-element.37) | copy-start | bytes 3460
  34.5 10.9 %copy-start.9 = (bf16[384,1536]{1,0:T(8,128)(2,1)S(1)}, bf16[384,1536]{1,0:T(8,128)(2,1)}, u32[]{:S(2)}) copy-start(bf16[384,1536]{1,0:T(8,128)(2,1)} %refs_11_.3) | copy-start | bytes 3538948
  34.5 10.9 %copy-start.11 = (bf16[1536,384]{1,0:T(8,128)(2,1)S(1)}, bf16[1536,384]{1,0:T(8,128)(2,1)}, u32[]{:S(2)}) copy-start(bf16[1536,384]{1,0:T(8,128)(2,1)} %refs_12_.3) | copy-start | bytes 3538948
  43.4 2.0 %copy-start.3 = (bf16[384,1152]{1,0:T(8,128)(2,1)S(1)}, bf16[384,1152]{1,0:T(8,128)(2,1)}, u32[]{:S(2)}) copy-start(bf16[384,1152]{1,0:T(8,128)(2,1)} %refs_8_.3) | copy-start | bytes 2654212
  43.6 8.8 %collective-permute-start.3 = (bf16[2,15,8,384]{3,2,1,0:T(8,128)(2,1)S(1)}, bf16[2,15,8,384]{3,2,1,0:T(8,128)(2,1)S(1)}, u32[]{:S(2)}, u32[]{:S(2)}) collective-permute-start(bf16[2,15,8,384]{3,2,1,0:T(8,128)(2,1)S(1)} %get-tuple-element.32), channel_id=1, source_target_pairs={{0,1},{1,2},{2,3},{3,0},{4,5},{5,6},{6,7},{7,4},{8,9},{9,10},{10,1... | collective-permute-start | bytes 552968 | tf_op jit(solution)/shard_map/ppermute | solution.py:223
  45.2 6.6 %collective-permute-start.4 = (bf16[2,3,24,384]{3,2,1,0:T(8,128)(2,1)S(1)}, bf16[2,3,24,384]{3,2,1,0:T(8,128)(2,1)S(1)}, u32[]{:S(2)}, u32[]{:S(2)}) collective-permute-start(bf16[2,3,24,384]{3,2,1,0:T(8,128)(2,1)S(1)} %get-tuple-element.33), channel_id=1, source_target_pairs={{0,4},{4,0},{1,5},{5,1},{2,6},{6,2},{3,7},{7,3},{8,12},{12,8},{9,1... | collective-permute-start | bytes 331784 | tf_op jit(solution)/shard_map/ppermute | solution.py:223
  45.2 6.6 %collective-permute-start.5 = (bf16[2,3,8,384]{3,2,1,0:T(8,128)(2,1)S(1)}, bf16[2,3,8,384]{3,2,1,0:T(8,128)(2,1)S(1)}, u32[]{:S(2)}, u32[]{:S(2)}) collective-permute-start(bf16[2,3,8,384]{3,2,1,0:T(8,128)(2,1)S(1)} %get-tuple-element.34), channel_id=1, source_target_pairs={{0,5},{1,6},{2,7},{3,4},{4,1},{5,2},{6,3},{7,0},{8,13},{9,14},{10,... | collective-permute-start | bytes 110600 | tf_op jit(solution)/shard_map/ppermute | solution.py:233
  (2 other events, 1.3 us)

commit v4 on v3

--- a/solution.py
+++ b/solution.py
@@ -28,10 +28,9 @@
 
 
 def bias_kernel(slab, with_rest, *refs):
-    main_idx, rest_idx, table, main_out, rest_a, rest_b = refs if with_rest else (
-        refs[0], None, refs[1], refs[2], None, None
-    )
+    main_idx, table, out = refs[0], refs[-2], refs[-1]
     tokens = main_idx.shape[0]
+    step = out.shape[0] // slab
     pieces = table.shape[0] // slab
     low = lax.broadcasted_iota(jnp.int32, (LO, LANES), 0)
 
@@ -56,10 +55,11 @@
         for start in range(0, 8, AT_ONCE):
             lines = [rows[start + line : start + line + 1] for line in range(AT_ONCE)]
             for line, values in enumerate(lookup(lines)):
-                main_out[pl.ds(block * 8 + start + line, slab, stride=tokens), :] = values
+                out[pl.ds(block * 8 + start + line, slab, stride=step), :] = values
 
     if not with_rest:
         return
+    rest_idx = refs[1]
     rest = rest_idx.shape[0]
 
     @pl.loop(0, rest // 8)
@@ -70,8 +70,8 @@
             for line in range(start, start + AT_ONCE // 2):
                 lines += [rows[line : line + 1, :LANES], rows[line : line + 1, LANES:]]
             for line, values in enumerate(lookup(lines)):
-                target = rest_b if line % 2 else rest_a
-                target[pl.ds(block * 8 + start + line // 2, slab, stride=rest), :] = values
+                base = tokens + rest * (line % 2)
+                out[pl.ds(base + block * 8 + start + line // 2, slab, stride=step), :] = values
 
 
 def bias_tables(earth_bias, bias_index):
@@ -87,13 +87,11 @@
     main_idx = bias_index[:LANES].T
     rest_idx = jnp.pad(bias_index[LANES:], ((0, 0), (0, 2 * LANES - tokens)))
     half = tokens // 2
-    main_shape = jax.ShapeDtypeStruct((slab * half, LANES), jnp.float32)
-    rest_shape = jax.ShapeDtypeStruct((slab * rest, LANES), jnp.float32)
-
-    def call(with_rest, shapes, *args):
+
+    def call(with_rest, rows, *args):
         return pl.pallas_call(
             functools.partial(bias_kernel, slab, with_rest),
-            out_shape=shapes,
+            out_shape=jax.ShapeDtypeStruct((slab * rows, LANES), jnp.float32),
             compiler_params=pltpu.CompilerParams(vmem_limit_bytes=GRANT // 2),
             cost_estimate=pl.CostEstimate(
                 flops=table.size * tokens * tokens, bytes_accessed=slab * tokens * tokens * 2,
@@ -102,11 +100,11 @@
             name="bias_lookup",
         )(*args, table)
 
-    first = call(False, main_shape, main_idx[:half])
-    return first, lambda: call(True, (main_shape, rest_shape, rest_shape), main_idx[half:], rest_idx)
-
-
-def attend_window(heads, normed, query, key, row, col, bias_first, bias_second, bias_a, bias_b, w_vt, turned):
+    first = call(False, half, main_idx[:half])
+    return first, lambda: call(True, half + 2 * rest, main_idx[half:], rest_idx)
+
+
+def attend_window(heads, normed, query, key, row, bias_first, bias_second, w_vt, turned):
     tokens, width = normed.shape
     dim = width // heads
     per = LANES // dim
@@ -114,6 +112,13 @@
     scale = dim ** (-0.5) * LOG2E
     value_t = lax.dot_general(w_vt[...], normed, NT, preferred_element_type=jnp.float32)
     value_t = value_t.astype(jnp.bfloat16)
+    row = row.astype(jnp.float32)
+    diagonal = lax.broadcasted_iota(jnp.int32, (tokens, tokens), 0) == lax.broadcasted_iota(
+        jnp.int32, (tokens, tokens), 1
+    )
+    col = jnp.sum(jnp.where(diagonal, row, 0.0), axis=1, keepdims=True)
+    half = tokens // 2
+    step = half + 2 * rest
     barred = jnp.where(col == row[:, :LANES], 0.0, -jnp.inf)
     owner = lax.broadcasted_iota(jnp.int32, (LANES, LANES), 1) // dim
     zero = jnp.zeros((), jnp.bfloat16)
@@ -125,8 +130,9 @@
         for h in range(per):
             head = group * per + h
             scores = raw[:, h * LANES : (h + 1) * LANES] * scale
-            span_of = slice(head * (tokens // 2), (head + 1) * (tokens // 2))
-            bias = jnp.concatenate([bias_first[span_of, :], bias_second[span_of, :]], axis=0)
+            bias = [bias_first[head * half : (head + 1) * half, :]]
+            bias += [bias_second[head * step : head * step + half, :]]
+            bias = jnp.concatenate(bias, axis=0)
             scores = scores + bias + barred
             grown = jnp.exp2(scores - jnp.max(scores, axis=0, keepdims=True))
             total = jnp.sum(grown, axis=0, keepdims=True)
@@ -140,7 +146,10 @@
     asked = query[LANES:]
     stacked = jnp.concatenate([jnp.where(owner == h, asked, zero) for h in range(heads)], axis=0)
     scores = lax.dot_general(stacked, key, NT, preferred_element_type=jnp.float32) * scale
-    scores = scores + jnp.concatenate([bias_a[...], bias_b[:, : tokens - LANES]], axis=1)
+    left = [bias_second[h * step + half : h * step + half + rest, :] for h in range(heads)]
+    right = [bias_second[h * step + half + rest : (h + 1) * step, :] for h in range(heads)]
+    left, right = jnp.concatenate(left, axis=0), jnp.concatenate(right, axis=0)
+    scores = scores + jnp.concatenate([left, right[:, : tokens - LANES]], axis=1)
     barred = jnp.where(col[LANES:] == row, 0.0, -jnp.inf)
     scores = scores + jnp.concatenate([barred] * heads, axis=0)
     grown = jnp.exp2(scores - jnp.max(scores, axis=1, keepdims=True))
@@ -155,22 +164,48 @@
     return jnp.concatenate([turned[...].T, last], axis=0).astype(jnp.bfloat16)
 
 
-def layer_kernel(heads, together, x, reg_row, reg_col, *refs):
-    biases, (w_qkv, w_vt, w_proj, w_fc1, w_fc2, out, turned) = refs[: 4 * together], refs[4 * together :]
+def layer_kernel(heads, together, x, *refs):
+    blocks, refs = refs[: 3 * together], refs[3 * together :]
+    away, out, turned, here, sems = refs[:5], refs[5], refs[6], refs[7:12], refs[12]
+    w_qkv, w_vt, w_proj, w_fc1, w_fc2 = here
+    away = (away[0].at[:, : w_qkv.shape[1]], *away[1:])
+    copies = [
+        pltpu.make_async_copy(source, target, sems.at[i])
+        for i, (source, target) in enumerate(zip(away, here))
+    ]
+    opening = pl.program_id(0) == 0
+
+    @pl.when(opening)
+    def _():
+        for copy in copies:
+            copy.start()
+
     tokens, width = x.shape[1:]
     fields = x[...].reshape(together * tokens, width)
     normed = norm_rows(fields)
-    packed = jnp.dot(normed, w_qkv[:, : 2 * width], preferred_element_type=jnp.float32)
+
+    @pl.when(opening)
+    def _():
+        copies[0].wait()
+        copies[1].wait()
+
+    packed = jnp.dot(normed, w_qkv[...], preferred_element_type=jnp.float32)
     packed = packed.astype(jnp.bfloat16)
     contexts = []
     for place in range(together):
         rows = slice(place * tokens, (place + 1) * tokens)
         contexts.append(
             attend_window(
-                heads, normed[rows], packed[rows, :width], packed[rows, width:], reg_row[place],
-                reg_col[place], *biases[4 * place : 4 * place + 4], w_vt, turned.at[place],
+                heads, normed[rows], packed[rows, :width], packed[rows, width:],
+                blocks[3 * place][0], *blocks[3 * place + 1 : 3 * place + 3], w_vt, turned.at[place],
             )
         )
+
+    @pl.when(opening)
+    def _():
+        for copy in copies[2:]:
+            copy.wait()
+
     context = jnp.concatenate(contexts, axis=0)
     projected = jnp.dot(context, w_proj[...], preferred_element_type=jnp.float32)
     projected = projected.astype(jnp.bfloat16).astype(jnp.float32)
@@ -182,17 +217,20 @@
     out[...] = summed.reshape(out.shape)
 
 
-def layer(windows, regions, tables, band_of, heads, w_qkv, w_vt, w_proj, w_fc1, w_fc2):
+def layer(windows, regions, tables, where_of, per_band, heads, w_qkv, w_vt, w_proj, w_fc1, w_fc2):
     count, tokens, width = windows.shape
-    rest = tokens - LANES
     together = 2 if count % 2 == 0 else 1
-    whole = lambda w: (0, 0)
-    bias_specs, bias_args = [], []
+    slab = -(-heads * (regions.shape[0] // per_band) // 8) * 8
+    specs, args = [], []
     for place in range(together):
-        band = lambda w, place=place: (band_of(w * together + place), 0)
-        for table, rows in zip(tables, (tokens // 2, tokens // 2, rest, rest)):
-            bias_specs.append(pl.BlockSpec((heads * rows, LANES), band))
-            bias_args.append(table)
+        window = lambda w, place=place: (where_of(w * together + place), 0, 0)
+        band = lambda w, place=place: (where_of(w * together + place) // per_band, 0)
+        specs.append(pl.BlockSpec((1, 1, tokens), window))
+        args.append(regions)
+        for table in tables:
+            rows = table.shape[0] // slab
+            specs.append(pl.BlockSpec((heads * rows, LANES), band))
+            args.append(table)
     weights = (w_qkv, w_vt, w_proj, w_fc1, w_fc2)
     return pl.pallas_call(
         functools.partial(layer_kernel, heads, together),
@@ -200,13 +238,16 @@
         out_shape=jax.ShapeDtypeStruct(windows.shape, jnp.float32),
         in_specs=[
             pl.BlockSpec((together, tokens, width), lambda w: (w, 0, 0)),
-            pl.BlockSpec((together, 1, tokens), lambda w: (w, 0, 0)),
-            pl.BlockSpec((together, tokens, 1), lambda w: (w, 0, 0)),
-            *bias_specs,
-            *[pl.BlockSpec(weight.shape, whole) for weight in weights],
+            *specs,
+            *[pl.BlockSpec(memory_space=pltpu.HBM)] * len(weights),
         ],
         out_specs=pl.BlockSpec((together, tokens, width), lambda w: (w, 0, 0)),
-        scratch_shapes=[pltpu.VMEM((together, width, LANES), jnp.float32)],
+        scratch_shapes=[
+            pltpu.VMEM((together, width, LANES), jnp.float32),
+            pltpu.VMEM((width, 2 * width), w_qkv.dtype),
+            *[pltpu.VMEM(weight.shape, weight.dtype) for weight in weights[1:]],
+            pltpu.SemaphoreType.DMA((len(weights),)),
+        ],
         compiler_params=pltpu.CompilerParams(vmem_limit_bytes=GRANT),
         cost_estimate=pl.CostEstimate(
             flops=2 * count * tokens * (w_qkv.size + w_proj.size + w_fc1.size + w_fc2.size) * 3,
@@ -214,7 +255,7 @@
             transcendentals=count * heads * tokens * tokens,
         ),
         name="layer",
-    )(windows, regions[:, None, :], regions[:, :, None], *bias_args, *weights)
+    )(windows, *args, *weights)
 
 
 def from_behind(value, axis, steps):
@@ -341,20 +382,21 @@
     cols = from_behind(halos[0], "lon", -1)
     rows = from_behind(halos[1], "lat", -1)
     corner = from_corner(halos[2], -1)
-    tables = (first, *second_call())
+    tables = (first, second_call())
     regions = region_ids.reshape(levels, lat_wins, WLAT, lon_wins, WLON)
-    regions = regions.transpose(1, 3, 0, 2, 4).reshape(lat_wins, lon_wins, tokens)
+    regions = regions.transpose(1, 3, 0, 2, 4).reshape(lat_wins * lon_wins, 1, tokens)
     counts = [lat_wins - 1 + lon_wins, (lat_wins - 1) * (lon_wins - 1)]
     window_shapes = tuple(
         jax.ShapeDtypeStruct((count, tokens, width), jnp.float32) for count in counts if count
     )
     windows = small(spread_kernel, window_shapes, "spread", fields, cols, rows, corner)
     weights = (w_qkv, w_qkv[:, 2 * width :].T, w_proj, w_fc1, w_fc2)
-    edge_regions = jnp.concatenate([regions[:-1, -1], regions[-1]], axis=0)
+    last = lat_wins - 1
     results = [
         layer(
-            windows[0], edge_regions, tables,
-            lambda w: jnp.minimum(w, lat_wins - 1), heads, *weights,
+            windows[0], regions, tables,
+            lambda w: jnp.where(w < last, (w + 1) * lon_wins - 1, last * lon_wins + w - last),
+            lon_wins, heads, *weights,
         )
     ]
     halos = small(
@@ -364,11 +406,11 @@
     rows = from_behind(halos[1], "lat", 1)
     corner = from_corner(halos[2], 1)
     if len(windows) > 1:
-        inner_regions = regions[:-1, :-1].reshape(-1, tokens)
+        inner = lon_wins - 1
         results.append(
             layer(
-                windows[1], inner_regions, tables,
-                lambda w: w // (lon_wins - 1), heads, *weights,
+                windows[1], regions, tables,
+                lambda w: w // inner * lon_wins + w % inner, lon_wins, heads, *weights,
             )
         )
     shape = jax.ShapeDtypeStruct(fields.shape, jnp.bfloat16)

time: 53.9 us -> 51 us (0.946)
  local copies, waits for them, and re-layouts: 15 us -> 10.1 us
  Pallas kernels: 28.1 us -> 29.9 us
    ppermute x4, starting transfers between devices: 6.77 us -> 1.94 us  [from_behind(): return lax.ppermute(value, axis, pairs)]
    ppermute x2, starting transfers between devices: 0.75 us -> 5.48 us  [from_corner(): return lax.ppermute(value, ('lat', 'lon'), pairs)]
    unnamed x37 -> x22, local copies, waits for them, and re-layouts: 10.9 us -> 7.49 us
    ppermute x4, waiting for transfers between devices: 0.57 us -> 3.06 us  [from_behind(): return lax.ppermute(value, axis, pairs)]
    ppermute x2, waiting for transfers between devices: 1.98 us -> 0.01 us  [from_corner(): return lax.ppermute(value, ('lat', 'lon'), pairs)]
    pallas_call x2, Pallas kernels: 13.2 us -> 15.1 us  [layer(): pl.pallas_call(functools.partial(layer_kernel, heads, together), grid=(co...]
    slice x2 -> x0, local copies, waits for them, and re-layouts: 1.33 us -> none  [the longest x1 0.72 us: local(): edge_regions = jnp.concatenate([regions[:-1, -1], regions[-1]], axis=0)]
    slice x2 -> x1, local copies, waits for them, and re-layouts: 0.01 us -> 0.98 us  [bias_tables(): main_idx = bias_index[:LANES].T]
  transfers between devices with their start and end apart: 6 -> 6, of which waited for: 2 -> 1; matrix products, arithmetic and copies ran while one was open for 5% -> 1% of each run, Pallas kernels for 21% -> 24%
where the time goes in v4:
time: 51 us; the launch traced here: 50.7 us
  Pallas kernels  29.9 us (59%)
  local copies, waits for them, and re-layouts  10.1 us (20%)
  starting transfers between devices  7.42 us (15%)
  waiting for transfers between devices  3.07 us (6%)
    pallas_call x2, Pallas kernels, layer(): pl.pallas_call(functools.partial(layer_kernel, heads, together), grid=(co...  15.1 us
    pallas_call x2, Pallas kernels, call(): pl.pallas_call(functools.partial(bias_kernel, slab, with_rest), out_shape...  11.8 us
    unnamed x22, local copies, waits for them, and re-layouts  7.49 us
    ppermute x2, starting transfers between devices, from_corner(): return lax.ppermute(value, ('lat', 'lon'), pairs)  5.48 us
    ppermute x4, waiting for transfers between devices, from_behind(): return lax.ppermute(value, axis, pairs)  3.06 us
    pallas_call x4, Pallas kernels, small(): pl.pallas_call(kernel, out_shape=shapes, compiler_params=pltpu.CompilerPa...  2.98 us
    ppermute x4, starting transfers between devices, from_behind(): return lax.ppermute(value, axis, pairs)  1.94 us
    reshape x1, local copies, waits for them, and re-layouts, bias_tables(): table = earth_bias.transpose(0, 2, 1).reshape(count, positions)  1.06 us
  transfers between devices with their start and end apart: 6, of which 1 were waited for; matrix products, arithmetic and copies ran while one was open for 1% of the time, Pallas kernels for 24%

profile of v4, /device:TPU:0, one launch (start us, length us, event | category | flops | bytes accessed | tf_op | source)
XLA Modules:
  0.0 50.7 jit_solution(1445408319017284099)
XLA Ops:
  0.0 1.0 %slice.15 = s32[128,144]{1,0:T(8,128)S(1)} slice(s32[144,144]{1,0:T(8,128)} %param.10), slice={[0:128], [0:144]} | slice | bytes 147456 | tf_op jit(solution)/shard_map/slice | solution.py:87
  1.1 1.1 %reshape.15 = bf16[36,3312]{1,0:T(8,128)(2,1)S(1)} reshape(bf16[3,12,3312]{2,1,0:T(8,128)(2,1)} %bitcast.15) | data formatting | bytes 476928 | tf_op jit(solution)/shard_map/reshape | solution.py:84
  2.2 0.2 reshape.16
  2.5 0.7 %pack.1 = (bf16[2,15,8,384]{3,2,1,0:T(8,128)(2,1)}, bf16[2,3,24,384]{3,2,1,0:T(8,128)(2,1)}, bf16[2,3,8,384]{3,2,1,0:T(8,128)(2,1)}) custom-call(bf16[2,18,24,384]{3,2,1,0:T(8,128)(2,1)S(1)} %copy-done.2), custom_call_target="tpu_custom_call" | custom-call | flops 331776 | bytes 1327104 | tf_op jit(solution)/shard_map/pack/pallas_call | solution.py:358
  3.2 5.0 %bias_lookup.2.refs_1_.refs_4_ = f32[2880,128]{1,0:T(8,128)S(1)} custom-call(s32[72,128]{1,0:T(8,128)S(1)} %get-tuple-element.30.refs_0_, bf16[520,256]{1,0:T(8,128)(2,1)S(1)} %bitcast.12), custom_call_target="tpu_custom_call" | custom-call | flops 2760376320 | bytes 1658880 | tf_op jit(solution)/shard_map/bias_lookup/pallas_call | solution.py:92
  8.2 1.1 %copy-done = f32[2880,128]{1,0:T(8,128)} copy-done((f32[2880,128]{1,0:T(8,128)}, f32[2880,128]{1,0:T(8,128)S(1)}, u32[]{:S(2)}) %copy-start) | copy-done | bytes 1474584
  9.4 4.5 %collective-permute-start.2 = (bf16[2,3,8,384]{3,2,1,0:T(8,128)(2,1)}, bf16[2,3,8,384]{3,2,1,0:T(8,128)(2,1)S(1)}, u32[]{:S(2)}, u32[]{:S(2)}) collective-permute-start(bf16[2,3,8,384]{3,2,1,0:T(8,128)(2,1)} %get-tuple-element.22), channel_id=1, source_target_pairs={{0,7},{1,4},{2,5},{3,6},{4,3},{5,0},{6,1},{7,2},{8,15},{9,12},{10,... | collective-permute-start | bytes 110600 | tf_op jit(solution)/shard_map/ppermute | solution.py:274
  13.9 0.7 %collective-permute-start.1 = (bf16[2,3,24,384]{3,2,1,0:T(8,128)(2,1)}, bf16[2,3,24,384]{3,2,1,0:T(8,128)(2,1)S(1)}, u32[]{:S(2)}, u32[]{:S(2)}) collective-permute-start(bf16[2,3,24,384]{3,2,1,0:T(8,128)(2,1)} %get-tuple-element.21), channel_id=1, source_target_pairs={{0,4},{4,0},{1,5},{5,1},{2,6},{6,2},{3,7},{7,3},{8,12},{12,8},{9,1... | collective-permute-start | bytes 331784 | tf_op jit(solution)/shard_map/ppermute | solution.py:264
  14.6 0.4 collective-permute-start
  15.0 6.9 %bias_lookup.3.refs_2_.refs_5_ = f32[4160,128]{1,0:T(8,128)S(1)} custom-call(s32[72,128]{1,0:T(8,128)S(1)} %get-tuple-element.29.refs_0_, s32[16,256]{1,0:T(8,128)S(1)} %pad.9.refs_1_, bf16[520,256]{1,0:T(8,128)(2,1)S(1)} %bitcast.13), custom_call_target="tpu_custom_call" | custom-call | flops 2760376320 | bytes 1658880 | tf_op jit(solution)/shard_map/bias_lookup/pallas_call | solution.py:92
  21.9 0.1 reshape.18
  22.1 0.2 copy.21
  22.4 1.1 %spread.1 = (f32[4,144,384]{2,1,0:T(8,128)S(1)}, f32[2,144,384]{2,1,0:T(8,128)S(1)}) custom-call(bf16[2,18,24,384]{3,2,1,0:T(8,128)(2,1)S(1)} %copy-done.2, bf16[2,15,8,384]{3,2,1,0:T(8,128)(2,1)} %collective-permute-done.cols, bf16[2,3,24,384]{3,2,1,0:T(8,128)(2,1)S(1)} %collective-permute-done.1.rows, bf16[2,3,8,384]{3,2,1,0:T(8,128)(2,1)S(1)} %collective-permute-done.2.corner), custom_call_target="tpu_custom_call" | custom-call | flops 497664 | bytes 1990656 | tf_op jit(solution)/shard_map/spread/pallas_call | solution.py:358
  23.5 1.4 %copy-done.1 = f32[2880,128]{1,0:T(8,128)S(1)} copy-done((f32[2880,128]{1,0:T(8,128)S(1)}, f32[2880,128]{1,0:T(8,128)}, u32[]{:S(2)}) %copy-start.1) | copy-done | bytes 1474584
  24.9 1.2 %copy-done.3 = bf16[384,1152]{1,0:T(8,128)(2,1)S(1)} copy-done((bf16[384,1152]{1,0:T(8,128)(2,1)S(1)}, bf16[384,1152]{1,0:T(8,128)(2,1)}, u32[]{:S(2)}) %copy-start.3) | copy-done | bytes 884760
  26.1 1.3 %copy-done.5 = bf16[384,1536]{1,0:T(8,128)(2,1)S(1)} copy-done((bf16[384,1536]{1,0:T(8,128)(2,1)S(1)}, bf16[384,1536]{1,0:T(8,128)(2,1)}, u32[]{:S(2)}) %copy-start.5) | copy-done | bytes 1179672
  27.3 1.3 %copy-done.7 = bf16[1536,384]{1,0:T(8,128)(2,1)S(1)} copy-done((bf16[1536,384]{1,0:T(8,128)(2,1)S(1)}, bf16[1536,384]{1,0:T(8,128)(2,1)}, u32[]{:S(2)}) %copy-start.7) | copy-done | bytes 1179672
  28.6 1.0 %copy-done.8 = bf16[384,384]{1,0:T(8,128)(2,1)S(1)} copy-done((bf16[384,384]{1,0:T(8,128)(2,1)S(1)}, bf16[384,384]{1,0:T(8,128)(2,1)}, u32[]{:S(2)}) %copy-start.8) | copy-done | bytes 294936
  29.6 9.9 %layer.2.edge.refs_0_ = f32[4,144,384]{2,1,0:T(8,128)S(1)} custom-call(f32[4,144,384]{2,1,0:T(8,128)S(1)} %get-tuple-element.23.x, s32[6,1,144]{2,1,0:T(1,128)S(1)} %reshape.20.refs_0_.refs_3_, f32[2880,128]{1,0:T(8,128)S(1)} %copy-done.1, f32[4160,128]{1,0:T(8,128)S(1)} %bias_lookup.3.refs_2_.refs_5_, s32[6,1,144]{2,1,0:T(1,128)S(1)} %reshape.20.refs_0_.refs_3_, ...), custom_call_target="tpu_custom_call" | custom-call | flops 6115295232 | bytes 5603328 | tf_op jit(solution)/shard_map/layer/pallas_call | solution.py:235
  39.6 1.0 %collective-permute-start.5 = (bf16[2,3,8,384]{3,2,1,0:T(8,128)(2,1)S(1)}, bf16[2,3,8,384]{3,2,1,0:T(8,128)(2,1)S(1)}, u32[]{:S(2)}, u32[]{:S(2)}) collective-permute-start(bf16[2,3,8,384]{3,2,1,0:T(8,128)(2,1)S(1)} %get-tuple-element.28), channel_id=1, source_target_pairs={{0,5},{1,6},{2,7},{3,4},{4,1},{5,2},{6,3},{7,0},{8,13},{9,14},{10,... | collective-permute-start | bytes 110600 | tf_op jit(solution)/shard_map/ppermute | solution.py:274
  40.5 0.8 %collective-permute-start.4 = (bf16[2,3,24,384]{3,2,1,0:T(8,128)(2,1)S(1)}, bf16[2,3,24,384]{3,2,1,0:T(8,128)(2,1)S(1)}, u32[]{:S(2)}, u32[]{:S(2)}) collective-permute-start(bf16[2,3,24,384]{3,2,1,0:T(8,128)(2,1)S(1)} %get-tuple-element.27), channel_id=1, source_target_pairs={{0,4},{4,0},{1,5},{5,1},{2,6},{6,2},{3,7},{7,3},{8,12},{12,8},{9,1... | collective-permute-start | bytes 331784 | tf_op jit(solution)/shard_map/ppermute | solution.py:264
  41.3 5.2 %layer.3.refs_1_ = f32[2,144,384]{2,1,0:T(8,128)S(1)} custom-call(f32[2,144,384]{2,1,0:T(8,128)S(1)} %get-tuple-element.25.x, s32[6,1,144]{2,1,0:T(1,128)S(1)} %reshape.20.refs_0_.refs_3_, f32[2880,128]{1,0:T(8,128)S(1)} %copy-done.1, f32[4160,128]{1,0:T(8,128)S(1)} %bias_lookup.3.refs_2_.refs_5_, s32[6,1,144]{2,1,0:T(1,128)S(1)} %reshape.20.refs_0_.refs_3_, ...), custom_call_target="tpu_custom_call" | custom-call | flops 3057647616 | bytes 5160960 | tf_op jit(solution)/shard_map/layer/pallas_call | solution.py:235
  46.6 3.1 %collective-permute-done.3.refs_2_ = bf16[2,15,8,384]{3,2,1,0:T(8,128)(2,1)S(1)} collective-permute-done((bf16[2,15,8,384]{3,2,1,0:T(8,128)(2,1)S(1)}, bf16[2,15,8,384]{3,2,1,0:T(8,128)(2,1)S(1)}, u32[]{:S(2)}, u32[]{:S(2)}) %collective-permute-start.3) | collective-permute-done | bytes 184352 | tf_op jit(solution)/shard_map/ppermute | solution.py:264
  49.7 1.0 %join.1 = bf16[2,18,24,384]{3,2,1,0:T(8,128)(2,1)} custom-call(f32[4,144,384]{2,1,0:T(8,128)S(1)} %layer.2.edge.refs_0_, f32[2,144,384]{2,1,0:T(8,128)S(1)} %layer.3.refs_1_, bf16[2,15,8,384]{3,2,1,0:T(8,128)(2,1)S(1)} %collective-permute-done.3.refs_2_, bf16[2,3,24,384]{3,2,1,0:T(8,128)(2,1)S(1)} %collective-permute-done.4.refs_3_, ...), custom_call_target="tpu_custom_call" | custom-call | flops 497664 | bytes 1990656 | tf_op jit(solution)/shard_map/join/pallas_call | solution.py:358
  (32 shorter events, 0.5 us)
Async XLA Ops:
  0.0 2.5 %copy-start.2 = (bf16[2,18,24,384]{3,2,1,0:T(8,128)(2,1)S(1)}, bf16[2,18,24,384]{3,2,1,0:T(8,128)(2,1)}, u32[]{:S(2)}) copy-start(bf16[2,18,24,384]{3,2,1,0:T(8,128)(2,1)} %fields.3) | copy-start | bytes 1990660
  3.2 11.8 %slice-start.1 = ((s32[144,144]{1,0:T(8,128)}), s32[16,144]{1,0:T(8,128)S(1)}, s32[]{:S(2)}) async-start(s32[144,144]{1,0:T(8,128)} %param.10), calls=%async_computation.1 | async-start | bytes 32768 | tf_op jit(solution)/shard_map/slice | solution.py:88
  8.2 1.1 %copy-start = (f32[2880,128]{1,0:T(8,128)}, f32[2880,128]{1,0:T(8,128)S(1)}, u32[]{:S(2)}) copy-start(f32[2880,128]{1,0:T(8,128)S(1)} %bias_lookup.2.refs_1_.refs_4_) | copy-start | bytes 4423684
  9.4 13.0 %collective-permute-start.2 = (bf16[2,3,8,384]{3,2,1,0:T(8,128)(2,1)}, bf16[2,3,8,384]{3,2,1,0:T(8,128)(2,1)S(1)}, u32[]{:S(2)}, u32[]{:S(2)}) collective-permute-start(bf16[2,3,8,384]{3,2,1,0:T(8,128)(2,1)} %get-tuple-element.22), channel_id=1, source_target_pairs={{0,7},{1,4},{2,5},{3,6},{4,3},{5,0},{6,1},{7,2},{8,15},{9,12},{10,... | collective-permute-start | bytes 110600 | tf_op jit(solution)/shard_map/ppermute | solution.py:274
  13.9 8.5 %collective-permute-start.1 = (bf16[2,3,24,384]{3,2,1,0:T(8,128)(2,1)}, bf16[2,3,24,384]{3,2,1,0:T(8,128)(2,1)S(1)}, u32[]{:S(2)}, u32[]{:S(2)}) collective-permute-start(bf16[2,3,24,384]{3,2,1,0:T(8,128)(2,1)} %get-tuple-element.21), channel_id=1, source_target_pairs={{0,4},{4,0},{1,5},{5,1},{2,6},{6,2},{3,7},{7,3},{8,12},{12,8},{9,1... | collective-permute-start | bytes 331784 | tf_op jit(solution)/shard_map/ppermute | solution.py:264
  14.6 7.8 %collective-permute-start = (bf16[2,15,8,384]{3,2,1,0:T(8,128)(2,1)}, bf16[2,15,8,384]{3,2,1,0:T(8,128)(2,1)}, u32[]{:S(2)}, u32[]{:S(2)}) collective-permute-start(bf16[2,15,8,384]{3,2,1,0:T(8,128)(2,1)} %get-tuple-element.20), channel_id=1, source_target_pairs={{0,3},{1,0},{2,1},{3,2},{4,7},{5,4},{6,5},{7,6},{8,11},{9,8},{10,9... | collective-permute-start | bytes 552968 | tf_op jit(solution)/shard_map/ppermute | solution.py:264
  15.0 6.9 %copy-start.9 = (s32[2,18,24]{2,0,1:T(2,128)S(1)}, s32[2,18,24]{2,0,1:T(2,128)}, u32[]{:S(2)}) copy-start(s32[2,18,24]{2,0,1:T(2,128)} %param.9) | copy-start | bytes 10372
  15.0 7.1 %slice-start = ((bf16[384,1152]{1,0:T(8,128)(2,1)}), bf16[384,384]{1,0:T(8,128)(2,1)S(1)}, s32[]{:S(2)}) async-start(bf16[384,1152]{1,0:T(8,128)(2,1)} %refs_6_.3), calls=%async_computation | async-start | bytes 589824 | tf_op jit(solution)/shard_map/slice | solution.py:393
  23.5 1.4 %copy-start.1 = (f32[2880,128]{1,0:T(8,128)S(1)}, f32[2880,128]{1,0:T(8,128)}, u32[]{:S(2)}) copy-start(f32[2880,128]{1,0:T(8,128)} %copy-done) | copy-start | bytes 4423684
  24.9 1.2 %copy-start.3 = (bf16[384,1152]{1,0:T(8,128)(2,1)S(1)}, bf16[384,1152]{1,0:T(8,128)(2,1)}, u32[]{:S(2)}) copy-start(bf16[384,1152]{1,0:T(8,128)(2,1)} %refs_6_.3) | copy-start | bytes 2654212
  26.1 1.3 %copy-start.5 = (bf16[384,1536]{1,0:T(8,128)(2,1)S(1)}, bf16[384,1536]{1,0:T(8,128)(2,1)}, u32[]{:S(2)}) copy-start(bf16[384,1536]{1,0:T(8,128)(2,1)} %refs_9_.3) | copy-start | bytes 3538948
  27.3 1.3 %copy-start.7 = (bf16[1536,384]{1,0:T(8,128)(2,1)S(1)}, bf16[1536,384]{1,0:T(8,128)(2,1)}, u32[]{:S(2)}) copy-start(bf16[1536,384]{1,0:T(8,128)(2,1)} %refs_10_.3) | copy-start | bytes 3538948
  28.6 1.0 %copy-start.8 = (bf16[384,384]{1,0:T(8,128)(2,1)S(1)}, bf16[384,384]{1,0:T(8,128)(2,1)}, u32[]{:S(2)}) copy-start(bf16[384,384]{1,0:T(8,128)(2,1)} %refs_8_.3) | copy-start | bytes 884740
  29.6 11.8 %copy-start.6 = (bf16[384,1536]{1,0:T(8,128)(2,1)S(1)}, bf16[384,1536]{1,0:T(8,128)(2,1)}, u32[]{:S(2)}) copy-start(bf16[384,1536]{1,0:T(8,128)(2,1)} %refs_9_.3) | copy-start | bytes 3538948
  39.5 1.9 %copy-start.4 = (bf16[384,1152]{1,0:T(8,128)(2,1)S(1)}, bf16[384,1152]{1,0:T(8,128)(2,1)}, u32[]{:S(2)}) copy-start(bf16[384,1152]{1,0:T(8,128)(2,1)} %refs_6_.3) | copy-start | bytes 2654212
  39.6 7.0 %collective-permute-start.5 = (bf16[2,3,8,384]{3,2,1,0:T(8,128)(2,1)S(1)}, bf16[2,3,8,384]{3,2,1,0:T(8,128)(2,1)S(1)}, u32[]{:S(2)}, u32[]{:S(2)}) collective-permute-start(bf16[2,3,8,384]{3,2,1,0:T(8,128)(2,1)S(1)} %get-tuple-element.28), channel_id=1, source_target_pairs={{0,5},{1,6},{2,7},{3,4},{4,1},{5,2},{6,3},{7,0},{8,13},{9,14},{10,... | collective-permute-start | bytes 110600 | tf_op jit(solution)/shard_map/ppermute | solution.py:274
  40.5 6.1 %collective-permute-start.4 = (bf16[2,3,24,384]{3,2,1,0:T(8,128)(2,1)S(1)}, bf16[2,3,24,384]{3,2,1,0:T(8,128)(2,1)S(1)}, u32[]{:S(2)}, u32[]{:S(2)}) collective-permute-start(bf16[2,3,24,384]{3,2,1,0:T(8,128)(2,1)S(1)} %get-tuple-element.27), channel_id=1, source_target_pairs={{0,4},{4,0},{1,5},{5,1},{2,6},{6,2},{3,7},{7,3},{8,12},{12,8},{9,1... | collective-permute-start | bytes 331784 | tf_op jit(solution)/shard_map/ppermute | solution.py:264
  41.3 8.3 %collective-permute-start.3 = (bf16[2,15,8,384]{3,2,1,0:T(8,128)(2,1)S(1)}, bf16[2,15,8,384]{3,2,1,0:T(8,128)(2,1)S(1)}, u32[]{:S(2)}, u32[]{:S(2)}) collective-permute-start(bf16[2,15,8,384]{3,2,1,0:T(8,128)(2,1)S(1)} %get-tuple-element.26), channel_id=1, source_target_pairs={{0,1},{1,2},{2,3},{3,0},{4,5},{5,6},{6,7},{7,4},{8,9},{9,10},{10,1... | collective-permute-start | bytes 552968 | tf_op jit(solution)/shard_map/ppermute | solution.py:264
